TPU v7x, 8 devices: a whole 2x2x1 slice. The times are simulated.
8 devices in a mesh: dp: 2 (over z, y), tp: 4 (over x, core).
Axes of the slice: x: 2, y: 2, z: 1, core: 2. Of those that a mesh axis runs over, the one named last changes fastest.
Arguments:
- layer_in: bfloat16 [4096, 1024], P(('dp', 'tp')), parts along dimension 0
- resid_mid: bfloat16 [4096, 1024], P(('dp', 'tp')), parts along dimension 0
- grad_out: bfloat16 [4096, 1024], P(('dp', 'tp')), parts along dimension 0
- ln1_gain: float32 [1024], replicated
- ln2_gain: float32 [1024], replicated
- w_qkv: bfloat16 [1024, 3072], P(None, 'tp')
- w_out: bfloat16 [16, 64, 1024], P('tp')
- w_fc1: bfloat16 [1024, 4096], P(None, 'tp')
- w_fc2: bfloat16 [4096, 1024], P('tp')
Outputs:
- output 1: bfloat16 [4096, 1024], P(('dp', 'tp')), parts along dimension 0
- output 2: bfloat16 [2048, 3072], P('dp', 'tp'), parts along dimension 0
- output 3: bfloat16 [32, 64, 1024], P(('dp', 'tp')), parts along dimension 0
- output 4: bfloat16 [2048, 4096], P('dp', 'tp'), parts along dimension 0
- output 5: bfloat16 [8192, 1024], P(('dp', 'tp')), parts along dimension 0
There are 2 independent parts. A program takes and returns all parts, laid end to end along the dimension named above; an argument that names none is the same for every part.
All inputs are finite; a program needn't handle non-finite values.
Results may differ from a plain program's by a relative error of at most 0.0151254.
Values are sent between devices in bfloat16 or wider.
A program may use at most 1 GiB of HBM per device.

v0:
```python
import jax
import jax.numpy as jnp
from jax import lax
from jax.sharding import PartitionSpec as P, NamedSharding

LN_EPS = 1e-5
GELU_COEF = 0.044715
GELU_SCALE = 0.7978845608028654


def ln_forward(rows):
    row_mean = jnp.mean(rows, axis=-1, keepdims=True)
    centered = rows - row_mean
    row_rstd = lax.rsqrt(jnp.mean(centered * centered, axis=-1, keepdims=True) + LN_EPS)
    return centered * row_rstd, row_rstd


def ln_backward(x_hat, row_rstd, ln_gain, grad_norm):
    grad_hat = grad_norm * ln_gain
    proj_one = jnp.mean(grad_hat, axis=-1, keepdims=True)
    proj_two = jnp.mean(grad_hat * x_hat, axis=-1, keepdims=True)
    return row_rstd * (grad_hat - proj_one - x_hat * proj_two)


def gelu_pair(pre_act):
    tanh_val = jnp.tanh(GELU_SCALE * (pre_act + GELU_COEF * pre_act * pre_act * pre_act))
    gelu_val = 0.5 * pre_act * (1.0 + tanh_val)
    gelu_der = 0.5 * (1.0 + tanh_val) + 0.5 * pre_act * (1.0 - tanh_val * tanh_val) * GELU_SCALE * (1.0 + 3.0 * GELU_COEF * pre_act * pre_act)
    return gelu_val, gelu_der


def attention_grads(norm_rows, grad_mid_rows, wqkv_part, wout_part):
    tokens = norm_rows.shape[0]
    heads_loc = wout_part.shape[0]
    head_dim = wout_part.shape[1]
    score_scale = head_dim ** -0.5
    qkv_rows = jnp.dot(norm_rows, wqkv_part, preferred_element_type=jnp.float32).astype(jnp.bfloat16)
    qkv_rows = qkv_rows.reshape(tokens, heads_loc, 3, head_dim)
    q_rows = qkv_rows[:, :, 0]
    k_rows = qkv_rows[:, :, 1]
    v_rows = qkv_rows[:, :, 2]
    scores = jnp.einsum('qnd,knd->nqk', q_rows, k_rows, preferred_element_type=jnp.float32) * score_scale
    causal = jnp.arange(tokens)[:, None] >= jnp.arange(tokens)[None, :]
    attn_prob = jax.nn.softmax(jnp.where(causal, scores, -1e30), axis=-1)
    prob_low = attn_prob.astype(jnp.bfloat16)
    attn_out = jnp.einsum('nqk,knd->qnd', prob_low, v_rows, preferred_element_type=jnp.float32).astype(jnp.bfloat16)
    grad_attn = jnp.einsum('tm,ndm->tnd', grad_mid_rows, wout_part, preferred_element_type=jnp.float32).astype(jnp.bfloat16)
    grad_v = jnp.einsum('nqk,qnd->knd', prob_low, grad_attn, preferred_element_type=jnp.float32).astype(jnp.bfloat16)
    grad_prob = jnp.einsum('qnd,knd->nqk', grad_attn, v_rows, preferred_element_type=jnp.float32)
    row_dot = jnp.sum(attn_prob * grad_prob, axis=-1, keepdims=True)
    grad_score = (attn_prob * (grad_prob - row_dot) * score_scale).astype(jnp.bfloat16)
    grad_q = jnp.einsum('nqk,knd->qnd', grad_score, k_rows, preferred_element_type=jnp.float32).astype(jnp.bfloat16)
    grad_k = jnp.einsum('nqk,qnd->knd', grad_score, q_rows, preferred_element_type=jnp.float32).astype(jnp.bfloat16)
    grad_qkv = jnp.stack([grad_q, grad_k, grad_v], axis=2).reshape(tokens, 3 * heads_loc * head_dim)
    return attn_out, grad_qkv


def solution(mesh):
    row_spec = P(('dp', 'tp'), None)
    in_specs = (row_spec, row_spec, row_spec, P(None), P(None), P(None, 'tp'), P('tp', None, None), P(None, 'tp'), P('tp', None))
    out_specs = (row_spec, P('dp', 'tp'), P(('dp', 'tp'), None, None), P('dp', 'tp'), P(('dp', 'tp'), None))

    def device_step(in_rows, mid_rows, gout_rows, ln1_gain, ln2_gain, wqkv_loc, wout_loc, wfc1_loc, wfc2_loc):
        mid_hat, mid_rstd = ln_forward(mid_rows.astype(jnp.float32))
        ln2_loc = (mid_hat * ln2_gain).astype(jnp.bfloat16)
        ln2_all = lax.all_gather(ln2_loc, 'tp', axis=0, tiled=True)
        gout_all = lax.all_gather(gout_rows, 'tp', axis=0, tiled=True)
        pre_act = jnp.dot(ln2_all, wfc1_loc, preferred_element_type=jnp.float32)
        gelu_val, gelu_der = gelu_pair(pre_act)
        act_low = gelu_val.astype(jnp.bfloat16)
        grad_wfc2 = jnp.einsum('tf,tm->fm', act_low, gout_all, preferred_element_type=jnp.float32).astype(jnp.bfloat16)
        grad_act = jnp.einsum('tm,fm->tf', gout_all, wfc2_loc, preferred_element_type=jnp.float32)
        grad_pre = (grad_act * gelu_der).astype(jnp.bfloat16)
        grad_wfc1 = jnp.einsum('tm,tf->mf', ln2_all, grad_pre, preferred_element_type=jnp.float32).astype(jnp.bfloat16)
        norm2_part = jnp.einsum('tf,mf->tm', grad_pre, wfc1_loc, preferred_element_type=jnp.float32).astype(jnp.bfloat16)
        grad_norm2 = lax.psum_scatter(norm2_part, 'tp', scatter_dimension=0, tiled=True)
        grad_mid = gout_rows.astype(jnp.float32) + ln_backward(mid_hat, mid_rstd, ln2_gain, grad_norm2.astype(jnp.float32))
        in_hat, in_rstd = ln_forward(in_rows.astype(jnp.float32))
        ln1_loc = (in_hat * ln1_gain).astype(jnp.bfloat16)
        ln1_all = lax.all_gather(ln1_loc, 'tp', axis=0, tiled=True)
        grad_mid_all = lax.all_gather(grad_mid.astype(jnp.bfloat16), 'tp', axis=0, tiled=True)
        attn_out, grad_qkv = attention_grads(ln1_all, grad_mid_all, wqkv_loc, wout_loc)
        grad_wout = jnp.einsum('tnd,tm->ndm', attn_out, grad_mid_all, preferred_element_type=jnp.float32).astype(jnp.bfloat16)
        grad_wqkv = jnp.einsum('tm,tc->mc', ln1_all, grad_qkv, preferred_element_type=jnp.float32).astype(jnp.bfloat16)
        norm1_part = jnp.einsum('tc,mc->tm', grad_qkv, wqkv_loc, preferred_element_type=jnp.float32).astype(jnp.bfloat16)
        grad_norm1 = lax.psum_scatter(norm1_part, 'tp', scatter_dimension=0, tiled=True)
        grad_in = (grad_mid + ln_backward(in_hat, in_rstd, ln1_gain, grad_norm1.astype(jnp.float32))).astype(jnp.bfloat16)
        return grad_in, grad_wqkv, grad_wout, grad_wfc1, grad_wfc2

    return jax.shard_map(device_step, mesh=mesh, in_specs=in_specs, out_specs=out_specs, check_vma=False)
```

profile of v0, /device:TPU:0, one launch (start us, length us, event | category | flops | bytes accessed | tf_op | source)
XLA Modules:
  0.0 502.9 jit_solution(10215589422501371532)
XLA Ops:
  7.2 0.0 all-gather.7.cloned.1.call-start
  7.2 1.6 convert_reduce_fusion.1
  8.8 1.6 fusion.84
  10.5 2.6 fusion.79
  13.1 0.0 all-gather.7.cloned.1.call-update
  13.1 0.0 all-gather.5.cloned.1.call-start
  13.1 0.7 all-gather.5.cloned.1.call-update
  13.8 0.0 reduce-scatter.3.cloned.1.call-start
  13.9 33.7 %all-gather.7.cloned.1.call-done = bf16[2048,1024]{1,0:T(8,128)(2,1)} async-done(((bf16[512,1024]{1,0:T(8,128)(2,1)}), bf16[2048,1024]{1,0:T(8,128)(2,1)}) %all-gather.7.cloned.1.call-update) | async-done | bytes 4194320 | tf_op jit(solution)/shard_map/all_gather | solution.py:66
  47.6 9.0 %fusion.107 = f32[2048,1024]{1,0:T(8,128)} fusion(bf16[2048,1024]{1,0:T(8,128)(2,1)} %all-gather.7.cloned.1.call-done, bf16[1024,1024]{1,0:T(8,128)(2,1)S(1)} %copy-done), kind=kOutput, calls=%fused_computation.108 | convolution fusion | flops 4294967296 | bytes 14680064 | tf_op jit(solution)/shard_map/dot_general | solution.py:68
  56.6 24.0 %all-gather.5.cloned.1.call-done = bf16[2048,1024]{1,0:T(8,128)(2,1)} async-done(((bf16[512,1024]{1,0:T(8,128)(2,1)}), bf16[2048,1024]{1,0:T(8,128)(2,1)}) %all-gather.5.cloned.1.call-update) | async-done | bytes 4194320 | tf_op jit(solution)/shard_map/all_gather | solution.py:67
  80.6 12.0 %fusion.25 = bf16[2048,1024]{1,0:T(8,128)(2,1)S(1)} fusion(f32[2048,1024]{1,0:T(8,128)} %fusion.107, bf16[2048,1024]{1,0:T(8,128)(2,1)} %all-gather.5.cloned.1.call-done, bf16[1024,1024]{1,0:T(8,128)(2,1)} %param.17), kind=kOutput, calls=%fused_computation.27 | convolution fusion | flops 4334813184 | bytes 18874368 | tf_op jit(solution)/shard_map/tm,fm->tf/dot_general | solution.py:72
  92.7 2.0 copy-done.28
  94.6 6.3 %convolution_convert_fusion.1 = bf16[2048,1024]{1,0:T(8,128)(2,1)} fusion(bf16[2048,1024]{1,0:T(8,128)(2,1)S(1)} %fusion.25, bf16[1024,1024]{1,0:T(8,128)(2,1)S(1)} %copy-done), kind=kOutput, calls=%fused_computation.36 | convolution fusion | flops 4297064448 | bytes 10485760 | tf_op jit(solution)/shard_map/tf,mf->tm/dot_general | solution.py:75
  101.0 0.0 reduce-scatter.3.cloned.1.call-update
  101.0 0.0 all-gather.9.cloned.1.call-start
  101.1 1.1 copy-done.4
  102.2 0.2 convert_reduce_fusion
  102.4 0.4 fusion.78
  102.9 1.3 fusion.72
  104.2 0.0 all-gather.9.cloned.1.call-update
  104.3 0.2 all-gather.11.cloned.1.call-start
  104.5 4.1 iota_compare_fusion
  108.6 8.1 %convolution_convert_fusion.3 = bf16[1024,1024]{1,0:T(8,128)(2,1)} fusion(bf16[2048,1024]{1,0:T(8,128)(2,1)S(1)} %copy-done.25, bf16[2048,1024]{1,0:T(8,128)(2,1)} %copy-done.28), kind=kOutput, calls=%fused_computation.79 | convolution fusion | flops 4296015872 | bytes 10485760 | tf_op jit(solution)/shard_map/tm,tf->mf/dot_general | solution.py:74
  116.7 22.7 %reduce-scatter.3.cloned.1.call-done = bf16[512,1024]{1,0:T(8,128)(2,1)} async-done(((bf16[2048,1024]{1,0:T(8,128)(2,1)}), bf16[512,1024]{1,0:T(8,128)(2,1)}) %reduce-scatter.3.cloned.1.call-update) | async-done | bytes 1048592 | tf_op jit(solution)/shard_map/reduce_scatter | solution.py:76
  139.5 2.0 fusion.86
  141.5 0.5 copy-done.20
  142.0 3.1 fusion.105
  145.1 0.0 reduce-scatter.5.cloned.1.call-start
  145.2 27.7 %all-gather.9.cloned.1.call-done = bf16[2048,1024]{1,0:T(8,128)(2,1)} async-done(((bf16[512,1024]{1,0:T(8,128)(2,1)}), bf16[2048,1024]{1,0:T(8,128)(2,1)}) %all-gather.9.cloned.1.call-update) | async-done | bytes 4194320 | tf_op jit(solution)/shard_map/all_gather | solution.py:80
  172.9 8.0 %convolution_convert_fusion.2 = bf16[2048,768]{0,1:T(8,128)(2,1)} fusion(bf16[2048,1024]{1,0:T(8,128)(2,1)} %all-gather.9.cloned.1.call-done, bf16[1024,768]{1,0:T(8,128)(2,1)} %param.14), kind=kOutput, calls=%fused_computation.37 | convolution fusion | flops 3222798336 | bytes 8912896 | tf_op jit(solution)/shard_map/dot_general | solution.py:37
  181.0 10.3 %fusion.87 = bf16[1024,1024]{1,0:T(8,128)(2,1)} fusion(bf16[2048,1024]{1,0:T(8,128)(2,1)S(1)} %copy-done.24, f32[2048,1024]{1,0:T(8,128)} %fusion.107), kind=kOutput, calls=%fused_computation.80 | convolution fusion | flops 4314890240 | bytes 14680064 | tf_op jit(solution)/shard_map/tf,tm->fm/dot_general | solution.py:71
  191.3 34.5 %fusion.106 = (f32[4,2048]{1,0:T(4,128)S(1)}, f32[4,2048,2048]{1,2,0:T(8,128)}) fusion(pred[2048,2048]{0,1:T(8,128)(4,1)} %iota_compare_fusion, bf16[2048,4,3,64]{0,3,2,1:T(8,128)(2,1)} %bitcast.90), kind=kOutput, calls=%fused_computation.107 | convolution fusion | flops 2214594560 | bytes 73433088 | tf_op jit(solution)/shard_map/sub | solution.py:44
  225.8 0.0 all-gather.11.cloned.1.call-done
  225.9 3.5 fusion.39
  229.3 24.5 %fusion.93 = f32[4,2048,2048]{1,2,0:T(8,128)} fusion(bf16[2048,4,64]{0,2,1:T(8,128)(2,1)S(1)} %fusion.39, bf16[2048,4,3,64]{0,3,2,1:T(8,128)(2,1)} %bitcast.91), kind=kOutput, calls=%fused_computation.86 | convolution fusion | flops 2147483648 | bytes 69206016 | tf_op jit(solution)/shard_map/qnd,knd->nqk/dot_general | solution.py:49
  253.8 24.1 %fusion.61 = bf16[2048,4,1,64]{0,3,1,2:T(8,128)(2,1)} fusion(bf16[2048,4,64]{0,2,1:T(8,128)(2,1)S(1)} %fusion.39, f32[4,2048,2048]{1,2,0:T(8,128)} %get-tuple-element.10, f32[4,2048]{1,0:T(4,128)S(1)} %get-tuple-element.9), kind=kOutput, calls=%fused_computation.59 | convolution fusion | flops 2181562368 | bytes 69238784 | tf_op jit(solution)/shard_map/nqk,qnd->knd/dot_general | solution.py:48
  277.9 82.8 %fusion.67 = bf16[2048,4,1,64]{0,3,1,2:T(8,128)(2,1)S(1)} fusion(f32[4,2048,2048]{1,2,0:T(8,128)} %fusion.93, bf16[2048,4,3,64]{0,3,2,1:T(8,128)(2,1)} %bitcast.92, f32[4,2048,2048]{1,2,0:T(8,128)} %get-tuple-element.10, f32[4,2048]{1,0:T(4,128)S(1)} %get-tuple-element.9), kind=kOutput, calls=%fused_computation.61 | convolution fusion | flops 2265458688 | bytes 270598144 | tf_op jit(solution)/shard_map/nqk,knd->qnd/dot_general | solution.py:52
  360.7 82.6 %fusion.64 = bf16[2048,4,1,64]{0,3,1,2:T(8,128)(2,1)S(1)} fusion(f32[4,2048,2048]{1,2,0:T(8,128)} %fusion.93, bf16[2048,4,3,64]{0,3,2,1:T(8,128)(2,1)} %bitcast.93, f32[4,2048,2048]{1,2,0:T(8,128)} %get-tuple-element.10, f32[4,2048]{1,0:T(4,128)S(1)} %get-tuple-element.9), kind=kOutput, calls=%fused_computation.60 | convolution fusion | flops 2265458688 | bytes 270598144 | tf_op jit(solution)/shard_map/nqk,qnd->knd/dot_general | solution.py:53
  443.3 0.3 pad_maximum_fusion
  443.7 0.4 copy.26
  444.1 1.6 copy-done.6
  445.7 5.3 %convolution_convert_fusion = bf16[2048,1024]{1,0:T(8,128)(2,1)} fusion(bf16[2048,768]{0,1:T(8,128)(2,1)S(1)} %bitcast.88, bf16[1024,768]{1,0:T(8,128)(2,1)S(1)} %copy-done.26), kind=kOutput, calls=%fused_computation.35 | convolution fusion | flops 3223322624 | bytes 8912896 | tf_op jit(solution)/shard_map/tc,mc->tm/dot_general | solution.py:85
  451.0 7.8 %convolution_convert_fusion.4 = bf16[1024,768]{1,0:T(8,128)(2,1)} fusion(bf16[2048,1024]{1,0:T(8,128)(2,1)} %all-gather.9.cloned.1.call-done, bf16[2048,768]{0,1:T(8,128)(2,1)} %bitcast.89), kind=kOutput, calls=%fused_computation.81 | convolution fusion | flops 3222011904 | bytes 8912896 | tf_op jit(solution)/shard_map/tm,tc->mc/dot_general | solution.py:84
  458.9 25.1 %fusion.88 = bf16[4,64,1024]{2,1,0:T(8,128)(2,1)} fusion(bf16[2048,1024]{1,0:T(8,128)(2,1)} %all-gather.11.cloned.1.call-done, bf16[2048,4,3,64]{0,3,2,1:T(8,128)(2,1)} %bitcast.94, f32[4,2048,2048]{1,2,0:T(8,128)} %get-tuple-element.10, f32[4,2048]{1,0:T(4,128)S(1)} %get-tuple-element.9), kind=kOutput, calls=%fused_computation.82 | convolution fusion | flops 3255566336 | bytes 72908800 | tf_op jit(solution)/shard_map/tnd,tm->ndm/dot_general | solution.py:83
  484.0 5.5 %reduce-scatter.5.cloned.1.call-done = bf16[512,1024]{1,0:T(8,128)(2,1)} async-done(((bf16[2048,1024]{1,0:T(8,128)(2,1)}), bf16[512,1024]{1,0:T(8,128)(2,1)}) %reduce-scatter.5.cloned.1.call-update) | async-done | bytes 1048592 | tf_op jit(solution)/shard_map/reduce_scatter | solution.py:86
  489.4 2.3 fusion.85
  491.8 4.1 fusion.77
  (63 shorter events, 0.2 us)
Async XLA Ops:
  7.2 40.4 %copy-start = (bf16[1024,1024]{1,0:T(8,128)(2,1)S(1)}, bf16[1024,1024]{1,0:T(8,128)(2,1)}, u32[]{:S(2)}) copy-start(bf16[1024,1024]{1,0:T(8,128)(2,1)} %param.16) | copy-start | bytes 6291460
  7.2 40.4 %all-gather.7.cloned.1.call-start = ((), (), s32[]{:S(2)}) async-start(), calls=%async_computation.3 | async-start | bytes 5242880 | tf_op jit(solution)/shard_map/all_gather | solution.py:66
  8.8 132.7 %copy-start.8 = (f32[512]{0:T(512)}, f32[512]{0:T(512)S(1)}, u32[]{:S(2)}) copy-start(f32[512]{0:T(512)S(1)} %broadcast_multiply_fusion.5) | copy-start | bytes 6148
  10.5 131.0 %copy-start.12 = (f32[512]{0:T(512)}, f32[512]{0:T(512)S(1)}, u32[]{:S(2)}) copy-start(f32[512]{0:T(512)S(1)} %add_rsqrt_fusion.1) | copy-start | bytes 6148
  13.1 67.5 %all-gather.5.cloned.1.call-start = ((), (), s32[]{:S(2)}) async-start(), calls=%async_computation.2 | async-start | bytes 5242880 | tf_op jit(solution)/shard_map/all_gather | solution.py:67
  13.8 125.6 %reduce-scatter.3.cloned.1.call-start = ((), (), s32[]{:S(2)}) async-start(), calls=%async_computation.4 | async-start | bytes 5242880 | tf_op jit(solution)/shard_map/reduce_scatter | solution.py:76
  92.7 2.0 copy-start.28
  101.0 1.2 copy-start.4
  101.0 1.9 copy-start.16
  101.0 71.9 %all-gather.9.cloned.1.call-start = ((), (), s32[]{:S(2)}) async-start(), calls=%async_computation.5 | async-start | bytes 5242880 | tf_op jit(solution)/shard_map/all_gather | solution.py:80
  102.4 2.1 copy-start.14
  102.9 1.6 copy-start.18
  104.3 121.6 %all-gather.11.cloned.1.call-start = ((), (), s32[]{:S(2)}) async-start(), calls=%async_computation.6 | async-start | bytes 5242880 | tf_op jit(solution)/shard_map/all_gather | solution.py:81
  104.5 4.1 copy-start.25
  108.6 30.8 %copy-start.2 = (bf16[512,1024]{1,0:T(8,128)(2,1)S(1)}, bf16[512,1024]{1,0:T(8,128)(2,1)}, u32[]{:S(2)}) copy-start(bf16[512,1024]{1,0:T(8,128)(2,1)} %param.10) | copy-start | bytes 3145732
  108.6 30.8 %copy-start.10 = (f32[1024]{0:T(1024)S(1)}, f32[1024]{0:T(1024)}, u32[]{:S(2)}) copy-start(f32[1024]{0:T(1024)} %param.13) | copy-start | bytes 12292
  108.6 33.4 %copy-start.5 = (bf16[512,1024]{1,0:T(8,128)(2,1)S(1)}, bf16[512,1024]{1,0:T(8,128)(2,1)}, u32[]{:S(2)}) copy-start(bf16[512,1024]{1,0:T(8,128)(2,1)} %param.11) | copy-start | bytes 3145732
  141.4 0.6 copy-start.20
  141.5 0.6 copy-start.22
  145.1 344.3 %reduce-scatter.5.cloned.1.call-start = ((), (), s32[]{:S(2)}) async-start(), calls=%async_computation.7 | async-start | bytes 5242880 | tf_op jit(solution)/shard_map/reduce_scatter | solution.py:86
  172.9 8.0 %copy-start.24 = (bf16[2048,1024]{1,0:T(8,128)(2,1)S(1)}, bf16[2048,1024]{1,0:T(8,128)(2,1)}, u32[]{:S(2)}) copy-start(bf16[2048,1024]{1,0:T(8,128)(2,1)} %all-gather.5.cloned.1.call-done) | copy-start | bytes 12582916
  191.3 34.6 %copy-start.27 = (bf16[4,64,1024]{2,1,0:T(8,128)(2,1)S(1)}, bf16[4,64,1024]{2,1,0:T(8,128)(2,1)}, u32[]{:S(2)}) copy-start(bf16[4,64,1024]{2,1,0:T(8,128)(2,1)} %param.15) | copy-start | bytes 1572868
  360.7 82.6 %copy-start.7 = (bf16[2048,4,1,64]{0,3,1,2:T(8,128)(2,1)S(1)}, bf16[2048,4,1,64]{0,3,1,2:T(8,128)(2,1)}, u32[]{:S(2)}) copy-start(bf16[2048,4,1,64]{0,3,1,2:T(8,128)(2,1)} %fusion.61) | copy-start | bytes 3145732
  443.7 2.0 copy-start.26
  444.1 1.6 copy-start.6
  458.8 30.6 %copy-start.15 = (f32[512]{0:T(512)S(1)}, f32[512]{0:T(512)}, u32[]{:S(2)}) copy-start(f32[512]{0:T(512)} %copy-done.14) | copy-start | bytes 6148
  458.8 30.6 %copy-start.17 = (f32[1024]{0:T(1024)S(1)}, f32[1024]{0:T(1024)}, u32[]{:S(2)}) copy-start(f32[1024]{0:T(1024)} %param.12) | copy-start | bytes 12292
  458.8 30.6 %copy-start.19 = (f32[512]{0:T(512)S(1)}, f32[512]{0:T(512)}, u32[]{:S(2)}) copy-start(f32[512]{0:T(512)} %copy-done.18) | copy-start | bytes 6148
  458.8 33.0 %copy-start.3 = (bf16[512,1024]{1,0:T(8,128)(2,1)S(1)}, bf16[512,1024]{1,0:T(8,128)(2,1)}, u32[]{:S(2)}) copy-start(bf16[512,1024]{1,0:T(8,128)(2,1)} %param.10) | copy-start | bytes 3145732
  458.8 33.0 %copy-start.9 = (f32[512]{0:T(512)S(1)}, f32[512]{0:T(512)}, u32[]{:S(2)}) copy-start(f32[512]{0:T(512)} %copy-done.8) | copy-start | bytes 6148
  458.8 33.0 %copy-start.11 = (f32[1024]{0:T(1024)S(1)}, f32[1024]{0:T(1024)}, u32[]{:S(2)}) copy-start(f32[1024]{0:T(1024)} %param.13) | copy-start | bytes 12292
  458.8 33.0 %copy-start.13 = (f32[512]{0:T(512)S(1)}, f32[512]{0:T(512)}, u32[]{:S(2)}) copy-start(f32[512]{0:T(512)} %copy-done.12) | copy-start | bytes 6148
  458.8 33.0 %copy-start.21 = (f32[512]{0:T(512)S(1)}, f32[512]{0:T(512)}, u32[]{:S(2)}) copy-start(f32[512]{0:T(512)} %copy-done.20) | copy-start | bytes 6148
  458.8 33.0 %copy-start.23 = (f32[512]{0:T(512)S(1)}, f32[512]{0:T(512)}, u32[]{:S(2)}) copy-start(f32[512]{0:T(512)} %copy-done.22) | copy-start | bytes 6148
  458.9 37.0 %copy-start.1 = (bf16[1024,1024]{1,0:T(8,128)(2,1)S(1)}, bf16[1024,1024]{1,0:T(8,128)(2,1)}, u32[]{:S(2)}) copy-start(bf16[1024,1024]{1,0:T(8,128)(2,1)} %param.16) | copy-start | bytes 6291460
Sparse Core Ops, SparseCore 0:
  13.2 34.3 all-gather.6
  49.1 31.4 all-gather.4
  101.1 38.2 reduce-scatter.2
  141.4 31.4 all-gather.8
  174.9 31.4 all-gather.10
  451.1 38.2 reduce-scatter.4
where the time goes:
time: 511 us; the launch traced here: 503 us
  matrix products  344 us (67%)
  waiting for transfers between devices  114 us (22%)
  other arithmetic  23.7 us (5%)
  between operations  14.6 us (3%)
  local copies, waits for them, and re-layouts  5.76 us (1%)
    dot_general x1, matrix products, attention_grads(): jnp.einsum('nqk,knd->qnd', grad_score, k_rows, preferred_element_type=jnp...  82.8 us
    dot_general x1, matrix products, attention_grads(): jnp.einsum('nqk,qnd->knd', grad_score, q_rows, preferred_element_type=jnp...  82.6 us
    sub x1, matrix products, attention_grads(): attn_prob = jax.nn.softmax(jnp.where(causal, scores, -1e+30), axis=-1)  34.5 us
    all_gather x1, waiting for transfers between devices, device_step(): ln2_all = lax.all_gather(ln2_loc, 'tp', axis=0, tiled=True)  33.7 us
    all_gather x1, waiting for transfers between devices, device_step(): ln1_all = lax.all_gather(ln1_loc, 'tp', axis=0, tiled=True)  27.7 us
    dot_general x1, matrix products, device_step(): jnp.einsum('tnd,tm->ndm', attn_out, grad_mid_all, preferred_element_type=...  25.1 us
    dot_general x1, matrix products, attention_grads(): jnp.einsum('qnd,knd->nqk', grad_attn, v_rows, preferred_element_type=jnp....  24.5 us
    dot_general x1, matrix products, attention_grads(): jnp.einsum('nqk,qnd->knd', prob_low, grad_attn, preferred_element_type=jn...  24.1 us
  transfers between devices with their start and end apart: 6, of which 5 were waited for; matrix products, arithmetic and copies ran while one was open for 23% of the time, Pallas kernels for 0%

commit v1 on v0

v1 whole, which is shorter than its diff:
```python
import jax
import jax.numpy as jnp
from jax import lax
from jax.experimental import pallas as pl
from jax.experimental.pallas import tpu as pltpu
from jax.sharding import PartitionSpec as P

LN_EPS = 1e-5
GELU_COEF = 0.044715
GELU_SCALE = 0.7978845608028654
LOG2E = 1.4426950408889634
F32 = jnp.float32
BF16 = jnp.bfloat16
BLK = 512
HALF = 256


def ln_forward(rows):
    row_mean = jnp.mean(rows, axis=-1, keepdims=True)
    centered = rows - row_mean
    row_rstd = lax.rsqrt(jnp.mean(centered * centered, axis=-1, keepdims=True) + LN_EPS)
    return centered * row_rstd, row_rstd


def ln_backward(x_hat, row_rstd, ln_gain, grad_norm):
    grad_hat = grad_norm * ln_gain
    proj_one = jnp.mean(grad_hat, axis=-1, keepdims=True)
    proj_two = jnp.mean(grad_hat * x_hat, axis=-1, keepdims=True)
    return row_rstd * (grad_hat - proj_one - x_hat * proj_two)


def gelu_pair(pre_act):
    tanh_val = jnp.tanh(GELU_SCALE * (pre_act + GELU_COEF * pre_act * pre_act * pre_act))
    gelu_val = 0.5 * pre_act * (1.0 + tanh_val)
    gelu_der = 0.5 * (1.0 + tanh_val) + 0.5 * pre_act * (1.0 - tanh_val * tanh_val) * GELU_SCALE * (1.0 + 3.0 * GELU_COEF * pre_act * pre_act)
    return gelu_val, gelu_der


def nn(a, b):
    return lax.dot_general(a, b, (((1,), (0,)), ((), ())), preferred_element_type=F32)


def nt(a, b):
    return lax.dot_general(a, b, (((1,), (1,)), ((), ())), preferred_element_type=F32)


def qkv_block(i, n1, wqkvt, ct, nat, nat_q):
    sl = pl.ds(pl.multiple_of(i * BLK, BLK), BLK)
    for n in range(4):
        c = nt(wqkvt[n * 192:(n + 1) * 192, :], n1[sl, :]).astype(BF16)
        q = c[0:64, :] * jnp.asarray(0.125, BF16)
        ct[n * 192:n * 192 + 64, sl] = q
        ct[n * 192 + 64:n * 192 + 192, sl] = c[64:192, :]
        nat_q[n, sl, :] = jnp.concatenate([q, jnp.zeros_like(q)], axis=0).T
        nat[2 * n, sl, :] = c[64:128, :].T
        nat[2 * n + 1, sl, :] = c[128:192, :].T


def fwd_init(ot, stat):
    ot[...] = jnp.zeros_like(ot)
    stat[0:4, :] = jnp.full((4, stat.shape[1]), -1e30, F32)
    stat[4:16, :] = jnp.zeros((12, stat.shape[1]), F32)


def fwd_tile(ki, qi, diag, ct, nat, ot, stat):
    qs = pl.ds(pl.multiple_of(qi * BLK, BLK), BLK)
    ks = pl.ds(pl.multiple_of(ki * BLK, BLK), BLK)
    for h in range(4):
        s = nn(nat[2 * h, ks, :], ct[3 * h * 64:3 * h * 64 + 64, qs])
        if diag:
            key = lax.broadcasted_iota(jnp.int32, (BLK, BLK), 0)
            query = lax.broadcasted_iota(jnp.int32, (BLK, BLK), 1)
            s = jnp.where(key <= query, s, -1e30)
        m_old = stat[h:h + 1, qs]
        m_new = jnp.maximum(m_old, jnp.max(s, axis=0, keepdims=True))
        alpha = jnp.exp2((m_old - m_new) * LOG2E)
        e = jnp.exp2((s - m_new) * LOG2E)
        stat[h:h + 1, qs] = m_new
        stat[4 + h:5 + h, qs] = stat[4 + h:5 + h, qs] * alpha + jnp.sum(e, axis=0, keepdims=True)
        hs = slice(h * 64, (h + 1) * 64)
        vt = ct[(3 * h + 2) * 64:(3 * h + 3) * 64, ks]
        ot[hs, qs] = ot[hs, qs] * alpha + nn(vt, e.astype(BF16))


def fwd_finish(ot, stat):
    for h in range(4):
        inv = 1.0 / stat[4 + h:5 + h, :]
        stat[4 + h:5 + h, :] = inv
        ot[h * 64:(h + 1) * 64, :] = ot[h * 64:(h + 1) * 64, :] * inv


def do_block(i, e, wo, ot, dot_t, nat_do, stat):
    sl = pl.ds(pl.multiple_of(i * BLK, BLK), BLK)
    d = nt(wo[...], e[sl, :]).astype(BF16)
    dot_t[:, sl] = d
    for h in range(4):
        part = d[h * 64:(h + 1) * 64, :]
        nat_do[h, sl, :] = jnp.concatenate([jnp.zeros_like(part), part], axis=0).T
        stat[8 + h:9 + h, sl] = jnp.sum(part.astype(F32) * ot[h * 64:(h + 1) * 64, sl], axis=0, keepdims=True)


def attn_bwd_tile(ki, qi, diag, ct, nat, nat_q, nat_do, dot_t, stat, dqt, dkv):
    ks = pl.ds(pl.multiple_of(ki * BLK, BLK), BLK)
    qs = pl.ds(pl.multiple_of(qi * BLK, BLK), BLK)
    for h in range(4):
        s = nn(nat[2 * h, ks, :], ct[3 * h * 64:3 * h * 64 + 64, qs])
        r = nn(nat[2 * h + 1, ks, :], dot_t[h * 64:(h + 1) * 64, qs])
        p = jnp.exp2((s - stat[h:h + 1, qs]) * LOG2E) * stat[4 + h:5 + h, qs]
        if diag:
            key = lax.broadcasted_iota(jnp.int32, (BLK, BLK), 0)
            query = lax.broadcasted_iota(jnp.int32, (BLK, BLK), 1)
            p = jnp.where(key <= query, p, 0.0)
        ds = (p * (r - stat[8 + h:9 + h, qs])).astype(BF16)
        dkv[h, ks, :] += nn(p.astype(BF16), nat_do[h, qs, :]) + nn(ds, nat_q[h, qs, :])
        hs = slice(h * 64, (h + 1) * 64)
        dqt[hs, qs] += nn(ct[(3 * h + 1) * 64:(3 * h + 2) * 64, ks], ds)


def pack_dc(i, dqt, dkv, dct):
    sl = pl.ds(pl.multiple_of(i * BLK, BLK), BLK)
    for h in range(4):
        dct[3 * h * 64:3 * h * 64 + 64, sl] = (dqt[h * 64:(h + 1) * 64, sl] * 0.125).astype(BF16)
        dct[(3 * h + 1) * 64:(3 * h + 3) * 64, sl] = dkv[h, sl, :].astype(BF16).T


MESH_ID = pl.DeviceIdType.MESH


def place():
    me = lax.axis_index('tp')
    chip = me // 2
    core = me - chip * 2
    return me, chip, core, chip * 2 + (1 - core), (1 - chip) * 2 + core, (1 - chip) * 2 + (1 - core)


def entry_barrier(others):
    barrier = pltpu.get_barrier_semaphore()
    for other in others:
        pl.semaphore_signal(barrier, inc=1, device_id={'tp': other}, device_id_type=MESH_ID)
    pl.semaphore_wait(barrier, 3)


def send(src, dst, ssem, rsem, to):
    return pltpu.make_async_remote_copy(src_ref=src, dst_ref=dst, send_sem=ssem, recv_sem=rsem, device_id={'tp': to}, device_id_type=MESH_ID)


def rows(start, size):
    return pl.ds(pl.multiple_of(start, size), size)


def tn(a, b):
    return lax.dot_general(a, b, (((0,), (0,)), ((), ())), preferred_element_type=F32)


def ln_rows(src, gain, dst, start):
    @pl.loop(0, 4)
    def _(i):
        hat, _ = ln_forward(src[rows(i * 128, 128), :].astype(F32))
        dst[rows(start + i * 128, 128), :] = (hat * gain[...]).astype(BF16)


def mlp_rows(start, n2, dy, w1, w2t, act, da):
    sl = rows(start, HALF)
    for c in range(4):
        cs = slice(c * 256, (c + 1) * 256)
        gelu_val, gelu_der = gelu_pair(nn(n2[sl, :], w1[:, cs]))
        act[sl, cs] = gelu_val.astype(BF16)
        da[sl, cs] = (nn(dy[sl, :], w2t[:, cs]) * gelu_der).astype(BF16)


def layer_kernel(h1_hbm, dy_hbm, x_hbm, g1, g2, wqkv_hbm, w1_hbm, w2_hbm, wo_hbm,
                 dx_hbm, dwqkv_hbm, dwo_hbm, dw1_hbm, dw2_hbm,
                 n2, dy, n1, w1_pair, da_pair, d2_send, d2_recv, d1_recv, w_pair, dct_far, dct_own, wqkvt, dh1, ct, nat, nat_q, ot, stat,
                 lsem, ssem, rsem, free_sem):
    me, chip, core, pair, peer, diag = place()
    own = rows(me * BLK, BLK)
    e = n2

    def chunk_copy(ref, block, n, first, to):
        sl = rows(block * BLK + n * HALF, HALF)
        return send(ref.at[sl, :], ref.at[sl, :], ssem.at[first + n], rsem.at[first + n], to)

    def d2_far(n):
        return send(d2_send.at[n], d2_recv.at[n], ssem.at[19 + n], rsem.at[19 + n], peer)

    def e_half(block, part_no):
        return e.at[rows(block * BLK + part_no * HALF, HALF), :]

    def e_pair(part_no):
        ref = e_half(me, part_no)
        return send(ref, ref, ssem.at[21 + part_no], rsem.at[21 + part_no], pair)

    def from_pair(part_no):
        ref = e_half(pair, part_no)
        return send(ref, ref, ssem.at[21 + part_no], rsem.at[21 + part_no], pair)

    def e_peer(n):
        ref = e_half(chip * 2 + 1 - n, core)
        return send(ref, ref, ssem.at[23 + n], rsem.at[23 + n], peer)

    def from_peer(n):
        ref = e_half((1 - chip) * 2 + 1 - n, core)
        return send(ref, ref, ssem.at[23 + n], rsem.at[23 + n], peer)

    def relay(n, part_no):
        ref = e_half((1 - chip) * 2 + 1 - n, part_no)
        return send(ref, ref, ssem.at[25 + n], rsem.at[25 + n], pair)

    w_swap = send(wqkvt, w_pair, ssem.at[29], rsem.at[29], pair)

    def phase_one(w1, w2t, wqkv, act, da, h1, x, dw1, dw2):
        local = []
        for n, (src, dst) in enumerate(((dy_hbm, dy.at[own, :]), (h1_hbm, h1), (x_hbm, x), (w1_hbm, w1), (w2_hbm, dw2), (wqkv_hbm, wqkv))):
            copy = pltpu.make_async_copy(src, dst, lsem.at[n])
            copy.start()
            local.append(copy)
        l_dy, l_h1, l_x, l_w1, l_w2, l_wqkv = local

        entry_barrier((pair, peer, diag))

        to_pair = [send(ref.at[own, :], ref.at[own, :], ssem.at[n], rsem.at[n], pair) for n, ref in enumerate((n2, dy, n1))]
        to_pair.append(send(w1, w1_pair, ssem.at[3], rsem.at[3], pair))
        l_dy.wait()
        chunk_copy(dy, me, 0, 6, peer).start()
        to_pair[1].start()
        l_h1.wait()
        ln_rows(h1, g2, n2, me * BLK)
        l_x.wait()
        ln_rows(x, g1, n1, me * BLK)
        chunk_copy(n2, me, 0, 4, peer).start()
        chunk_copy(dy, me, 1, 6, peer).start()
        chunk_copy(n2, me, 1, 4, peer).start()
        for n in range(2):
            chunk_copy(n1, me, n, 8, peer).start()
        to_pair[0].start()
        to_pair[2].start()
        l_w1.wait()
        to_pair[3].start()

        l_w2.wait()
        w2t[...] = dw2[...].T

        @pl.loop(0, 4)
        def _(i):
            @pl.when(i == 2)
            def _():
                to_pair[0].wait_recv()
                to_pair[1].wait_recv()

            second = i // 2
            mlp_rows((me + second * (pair - me)) * BLK + (i - 2 * second) * HALF, n2, dy, w1, w2t, act, da)

        da_swap = send(da.at[rows(pair * BLK, BLK), :], da_pair.at[0:BLK, :], ssem.at[16], rsem.at[16], pair)
        da_swap.start()
        l_wqkv.wait()
        wqkvt[...] = wqkv[...].T
        fwd_init(ot, stat)
        to_pair[2].wait_recv()

        @pl.loop(0, 2)
        def _(n):
            qkv_block(chip * 2 + n, n1, wqkvt, ct, nat, nat_q)

        w_swap.start()

        def da_far(n):
            return send(da.at[rows(diag * BLK + n * HALF, HALF), :], da_pair.at[rows(BLK + n * HALF, HALF), :], ssem.at[17 + n], rsem.at[17 + n], pair)

        to_pair[3].wait_recv()

        @pl.loop(0, 2)
        def _(n):
            chunk_copy(dy, peer, n, 6, peer).wait_recv()
            chunk_copy(dy, peer, n, 12, pair).start()
            chunk_copy(n2, peer, n, 4, peer).wait_recv()
            chunk_copy(n2, peer, n, 10, pair).start()

            @pl.loop(0, 2)
            def _(j):
                @pl.when(j == 1)
                def _():
                    chunk_copy(n2, diag, n, 10, pair).wait_recv()
                    chunk_copy(dy, diag, n, 12, pair).wait_recv()

                mlp_rows((peer + j * (diag - peer)) * BLK + n * HALF, n2, dy, w1, w2t, act, da)

            da_far(n).start()
            first = nt(da[rows(peer * BLK + n * HALF, HALF), :], w1[...])
            da_far(n).wait_recv()
            d2_send[n] = (first + nt(da_pair[rows(BLK + n * HALF, HALF), :], w1_pair[...])).astype(BF16)
            d2_far(n).start()

        da_swap.wait_recv()

        @pl.loop(0, 2)
        def _(i):
            sl = rows(i * HALF, HALF)
            dh1[sl, :] = nt(da[rows(me * BLK + i * HALF, HALF), :], w1[...]) + nt(da_pair[sl, :], w1_pair[...])

        outs = [pltpu.make_async_copy(src, dst, lsem.at[6 + n]) for n, (src, dst) in enumerate(((dw1, dw1_hbm), (dw2, dw2_hbm)))]

        @pl.loop(0, 6)
        def _(i):
            @pl.when(i == 2)
            def _():
                @pl.loop(0, 4)
                def _(j):
                    sl = rows(j * 256, 256)
                    dw2[sl, :] = tn(act[:, sl], dy[...]).astype(BF16)
                    dw1[sl, :] = tn(n2[:, sl], da[...]).astype(BF16)

                for copy in outs:
                    copy.start()
                to_pair[0].wait_send()
                for n in range(2):
                    chunk_copy(n2, me, n, 4, peer).wait_send()
                    chunk_copy(n2, peer, n, 10, pair).wait_send()
                for other in (pair, peer):
                    pl.semaphore_signal(free_sem, inc=1, device_id={'tp': other}, device_id_type=MESH_ID)
                for n in range(2):
                    chunk_copy(n1, peer, n, 8, peer).wait_recv()
                    chunk_copy(n1, peer, n, 14, pair).start()

                @pl.loop(0, 2)
                def _(j):
                    @pl.when(j == 1)
                    def _():
                        for n in range(2):
                            chunk_copy(n1, diag, n, 14, pair).wait_recv()

                    qkv_block(peer + j * (diag - peer), n1, wqkvt, ct, nat, nat_q)

            group = i // 2
            far = group % 2
            qi = far * 2 + chip * 2 - 4 * far * chip + i - 2 * group
            low = (1 - far) * (1 - group // 2) * chip * 2
            high = qi + (group // 2) * (chip * 2 - qi)

            @pl.loop(low, high)
            def _(ki):
                fwd_tile(ki, qi, False, ct, nat, ot, stat)

            @pl.when(group < 2)
            def _():
                fwd_tile(qi, qi, True, ct, nat, ot, stat)

        fwd_finish(ot, stat)
        for copy in outs:
            copy.wait()
        for copy in to_pair[1:] + [da_swap]:
            copy.wait_send()
        for n in range(2):
            for ref, block, first, to in ((dy, me, 6, peer), (n1, me, 8, peer), (dy, peer, 12, pair), (n1, peer, 14, pair)):
                chunk_copy(ref, block, n, first, to).wait_send()
            da_far(n).wait_send()
        pl.semaphore_wait(free_sem, 2)

        @pl.loop(0, 2)
        def _(n):
            d2_far(n).wait_recv()
            sl = rows(n * HALF, HALF)
            hat, rstd = ln_forward(h1[sl, :].astype(F32))
            rows_n = rows(me * BLK + n * HALF, HALF)
            grad = dy[rows_n, :].astype(F32) + ln_backward(hat, rstd, g2[...], dh1[sl, :] + d2_recv[n].astype(F32))
            dh1[sl, :] = grad
            e[rows_n, :] = grad.astype(BF16)
            e_pair(n).start()

            @pl.when(core == n)
            def _():
                @pl.when(core == 1)
                def _():
                    e_peer(0).start()

                from_pair(core).wait_recv()

                @pl.when(core == 0)
                def _():
                    e_peer(0).start()

                e_peer(1).start()

    pl.run_scoped(
        phase_one,
        w1=pltpu.VMEM((1024, 1024), BF16),
        w2t=pltpu.VMEM((1024, 1024), BF16),
        wqkv=pltpu.VMEM((1024, 768), BF16),
        act=pltpu.VMEM((4 * BLK, 1024), BF16),
        da=pltpu.VMEM((4 * BLK, 1024), BF16),
        h1=pltpu.VMEM((BLK, 1024), BF16),
        x=pltpu.VMEM((BLK, 1024), BF16),
        dw1=pltpu.VMEM((1024, 1024), BF16),
        dw2=pltpu.VMEM((1024, 1024), BF16),
    )

    def phase_two(nat_do, dot_t, dqt, dkv, wo, part, x, dx, dwqkv, dwo, dct):
        l_wo = pltpu.make_async_copy(wo_hbm, wo, lsem.at[8])
        l_wo.start()
        l_x = pltpu.make_async_copy(x_hbm, x, lsem.at[9])
        l_x.start()
        dkv[...] = jnp.zeros_like(dkv)
        dqt[...] = jnp.zeros_like(dqt)
        from_pair(1 - core).wait_recv()
        for n in range(2):
            d2_far(n).wait_send()
        l_wo.wait()

        @pl.loop(0, 2)
        def _(n):
            do_block(chip * 2 + n, e, wo, ot, dot_t, nat_do, stat)

        w_swap.wait_recv()

        def swap_far(n, mine_or_theirs):
            block = (1 - chip) * 2 + 1 - n
            return send(dct.at[:, rows(block * BLK + mine_or_theirs * HALF, HALF)], dct_far.at[n], ssem.at[27 + n], rsem.at[27 + n], pair)

        def d1_far(n):
            return send(d2_send.at[n], d1_recv.at[core], ssem.at[30 + n], rsem.at[30 + core], (1 - chip) * 2 + 1 - n)

        @pl.loop(0, 6)
        def _(i):
            group = i // 2
            far = group % 2
            n = i - 2 * group
            qi = (1 - far) * (chip * 2 + n) + far * ((1 - chip) * 2 + 1 - n)
            low = (group // 2) * chip * 2
            high = far * qi + (1 - far) * ((1 - group // 2) * ((1 - chip) * qi + chip * 2) + (group // 2) * chip * qi)

            @pl.when(far == 1)
            def _():
                from_peer(n).wait_recv()
                relay(n, core).start()
                relay(n, 1 - core).wait_recv()
                do_block(qi, e, wo, ot, dot_t, nat_do, stat)

            @pl.loop(low, high)
            def _(ki):
                attn_bwd_tile(ki, qi, False, ct, nat, nat_q, nat_do, dot_t, stat, dqt, dkv)

            @pl.when(far + (1 - far) * ((1 - group // 2) * (1 - chip) + (group // 2) * chip) == 1)
            def _():
                attn_bwd_tile(qi, qi, True, ct, nat, nat_q, nat_do, dot_t, stat, dqt, dkv)

            @pl.when(far == 1)
            def _():
                pack_dc(qi, dqt, dkv, dct)
                swap_far(n, 1 - core).start()
                part[0:HALF, :] = nn(dct[:, rows(qi * BLK + core * HALF, HALF)].T, wqkvt[...])
                swap_far(n, core).wait_recv()
                d2_send[n] = (part[0:HALF, :] + nn(dct_far[n].T, w_pair[...])).astype(BF16)
                d1_far(n).start()

        @pl.loop(0, 2)
        def _(n):
            pack_dc(chip * 2 + n, dqt, dkv, dct)

        swap = send(dct.at[:, rows(pair * BLK, BLK)], dct_own, ssem.at[32], rsem.at[32], pair)
        swap.start()
        part[...] = nn(dct[:, own].T, wqkvt[...])
        swap.wait_recv()
        part[...] += nn(dct_own[...].T, w_pair[...])

        @pl.loop(0, 4)
        def _(i):
            sl = rows(i * 256, 256)
            dwo[:, sl] = nn(ot[...].astype(BF16), e[:, sl]).astype(BF16)
            dwqkv[sl, :] = nn(dct[...], n1[:, sl]).astype(BF16).T

        outs = [pltpu.make_async_copy(src, dst, lsem.at[10 + n]) for n, (src, dst) in enumerate(((dwqkv, dwqkv_hbm), (dwo, dwo_hbm), (dx, dx_hbm)))]
        outs[0].start()
        outs[1].start()
        l_x.wait()

        @pl.loop(0, 2)
        def _(n):
            send(d2_send.at[n], d1_recv.at[n], ssem.at[30 + n], rsem.at[30 + n], peer).wait_recv()
            sl = rows(n * HALF, HALF)
            hat, rstd = ln_forward(x[sl, :].astype(F32))
            grad = part[sl, :] + d1_recv[n].astype(F32)
            dx[sl, :] = (dh1[sl, :] + ln_backward(hat, rstd, g1[...], grad)).astype(BF16)

        outs[2].start()
        for n in range(2):
            e_pair(n).wait_send()
            e_peer(n).wait_send()
            relay(n, core).wait_send()
            swap_far(n, 1 - core).wait_send()
            d1_far(n).wait_send()
        w_swap.wait_send()
        swap.wait_send()
        for copy in outs:
            copy.wait()

    tokens = 4 * BLK
    pl.run_scoped(
        phase_two,
        nat_do=pltpu.VMEM((4, tokens, 128), BF16),
        dot_t=pltpu.VMEM((256, tokens), BF16),
        dqt=pltpu.VMEM((256, tokens), F32),
        dkv=pltpu.VMEM((4, tokens, 128), F32),
        wo=pltpu.VMEM((256, 1024), BF16),
        part=pltpu.VMEM((BLK, 1024), F32),
        x=pltpu.VMEM((BLK, 1024), BF16),
        dx=pltpu.VMEM((BLK, 1024), BF16),
        dwqkv=pltpu.VMEM((1024, 768), BF16),
        dwo=pltpu.VMEM((256, 1024), BF16),
        dct=pltpu.VMEM((768, tokens), BF16),
    )


def layer_grads(h1, dy, x, g1, g2, wqkv, w1, w2, wo):
    tokens = 4 * BLK
    vmem = pltpu.VMEM
    shape = jax.ShapeDtypeStruct
    hbm = pl.BlockSpec(memory_space=pl.ANY)
    return pl.pallas_call(
        layer_kernel,
        name="layer_grads",
        out_shape=(shape((BLK, 1024), BF16), shape((1024, 768), BF16), shape((256, 1024), BF16), shape((1024, 1024), BF16), shape((1024, 1024), BF16)),
        in_specs=[hbm] * 3 + [pl.BlockSpec(memory_space=vmem)] * 2 + [hbm] * 4,
        out_specs=[hbm] * 5,
        scratch_shapes=[
            vmem((tokens, 1024), BF16),
            vmem((tokens, 1024), BF16),
            vmem((tokens, 1024), BF16),
            vmem((1024, 1024), BF16),
            vmem((2 * BLK, 1024), BF16),
            vmem((2, HALF, 1024), BF16),
            vmem((2, HALF, 1024), BF16),
            vmem((2, HALF, 1024), BF16),
            vmem((768, 1024), BF16),
            vmem((2, 768, HALF), BF16),
            vmem((768, BLK), BF16),
            vmem((768, 1024), BF16),
            vmem((BLK, 1024), F32),
            vmem((768, tokens), BF16),
            vmem((8, tokens, 64), BF16),
            vmem((4, tokens, 128), BF16),
            vmem((256, tokens), F32),
            vmem((16, tokens), F32),
            pltpu.SemaphoreType.DMA((13,)),
            pltpu.SemaphoreType.DMA((33,)),
            pltpu.SemaphoreType.DMA((33,)),
            pltpu.SemaphoreType.REGULAR,
        ],
        compiler_params=pltpu.CompilerParams(collective_id=0, has_side_effects=True, vmem_limit_bytes=67043328),
        cost_estimate=pl.CostEstimate(flops=80_000_000_000, bytes_accessed=40_000_000, transcendentals=40_000_000),
    )(h1, dy, x, g1, g2, wqkv, w1, w2, wo)


def solution(mesh):
    row_spec = P(('dp', 'tp'), None)
    in_specs = (row_spec, row_spec, row_spec, P(None), P(None), P(None, 'tp'), P('tp', None, None), P(None, 'tp'), P('tp', None))
    out_specs = (row_spec, P('dp', 'tp'), P(('dp', 'tp'), None, None), P('dp', 'tp'), P(('dp', 'tp'), None))

    def device_step(in_rows, mid_rows, gout_rows, ln1_gain, ln2_gain, wqkv_loc, wout_loc, wfc1_loc, wfc2_loc):
        grad_in, grad_wqkv, grad_wout, grad_wfc1, grad_wfc2 = layer_grads(mid_rows, gout_rows, in_rows, ln1_gain.reshape(1, 1024), ln2_gain.reshape(1, 1024), wqkv_loc, wfc1_loc, wfc2_loc, wout_loc.reshape(256, 1024))
        return grad_in, grad_wqkv, grad_wout.reshape(4, 64, 1024), grad_wfc1, grad_wfc2

    return jax.shard_map(device_step, mesh=mesh, in_specs=in_specs, out_specs=out_specs, check_vma=False)
```

time: 511 us -> 162 us (0.32)
  the two profiles are of different devices: /device:TPU:0 before, /device:TPU:2 now
where the time goes in v1:
time: 162 us
  Pallas kernels  153 us (94%)
  local copies, waits for them, and re-layouts  8.38 us (5%)
    pallas_call x1, Pallas kernels, layer_grads(): pl.pallas_call(layer_kernel, name='layer_grads', out_shape=(shape((BLK, 1...  153 us
    unnamed x13, local copies, waits for them, and re-layouts  8.38 us

profile of v1, /device:TPU:2, one launch (start us, length us, event | category | flops | bytes accessed | tf_op | source)
XLA Modules:
  0.0 161.7 jit_solution(949359824020446310)
XLA Ops:
  0.6 152.6 %layer_grads.1 = (bf16[512,1024]{1,0:T(8,128)(2,1)}, bf16[1024,768]{1,0:T(8,128)(2,1)}, bf16[256,1024]{1,0:T(8,128)(2,1)}, bf16[1024,1024]{1,0:T(8,128)(2,1)}, bf16[1024,1024]{1,0:T(8,128)(2,1)}) custom-call(bf16[512,1024]{1,0:T(8,128)(2,1)} %h1_hbm.1, bf16[512,1024]{1,0:T(8,128)(2,1)} %dy_hbm.1, bf16[512,1024]{1,0:T(8,128)(2,1)} %x_hbm.1, ...), custom_call_target="tpu_custom_call" | custom-call | flops 80000000000 | bytes 40000000 | tf_op jit(solution)/shard_map/layer_grads/pallas_call | solution.py:517
  153.3 0.0 copy-start.2
  153.3 2.4 %copy.19 = bf16[512,1024]{1,0:T(8,128)(2,1)} copy(bf16[512,1024]{1,0:T(8,128)(2,1)} %get-tuple-element.20) | data formatting | bytes 2097152
  155.7 0.0 copy-done.2
  155.7 0.0 copy-start.3
  155.7 0.0 copy-start.1
  155.7 1.1 copy.20
  156.8 0.2 copy-done.3
  157.1 0.8 copy.21
  157.8 0.2 copy-done.1
  158.0 0.0 copy-start
  158.0 1.3 copy.22
  159.3 1.0 copy-done
  160.4 1.3 copy.23
Async XLA Ops:
  153.3 2.4 %copy-start.2 = (bf16[1024,768]{1,0:T(8,128)(2,1)S(1)}, bf16[1024,768]{1,0:T(8,128)(2,1)}, u32[]{:S(2)}) copy-start(bf16[1024,768]{1,0:T(8,128)(2,1)} %get-tuple-element.21) | copy-start | bytes 4718596
  155.7 1.4 copy-start.3
  155.7 2.3 %copy-start.1 = (bf16[1024,1024]{1,0:T(8,128)(2,1)S(1)}, bf16[1024,1024]{1,0:T(8,128)(2,1)}, u32[]{:S(2)}) copy-start(bf16[1024,1024]{1,0:T(8,128)(2,1)} %get-tuple-element.23) | copy-start | bytes 6291460
  158.0 2.3 %copy-start = (bf16[1024,1024]{1,0:T(8,128)(2,1)S(1)}, bf16[1024,1024]{1,0:T(8,128)(2,1)}, u32[]{:S(2)}) copy-start(bf16[1024,1024]{1,0:T(8,128)(2,1)} %get-tuple-element.24) | copy-start | bytes 6291460

commit v2 on v1

--- a/solution.py
+++ b/solution.py
@@ -90,7 +90,7 @@
 
 
 def do_block(i, e, wo, ot, dot_t, nat_do, stat):
-    sl = pl.ds(pl.multiple_of(i * BLK, BLK), BLK)
+    sl = pl.ds(pl.multiple_of(i * HALF, HALF), HALF)
     d = nt(wo[...], e[sl, :]).astype(BF16)
     dot_t[:, sl] = d
     for h in range(4):
@@ -99,16 +99,16 @@
         stat[8 + h:9 + h, sl] = jnp.sum(part.astype(F32) * ot[h * 64:(h + 1) * 64, sl], axis=0, keepdims=True)
 
 
-def attn_bwd_tile(ki, qi, diag, ct, nat, nat_q, nat_do, dot_t, stat, dqt, dkv):
-    ks = pl.ds(pl.multiple_of(ki * BLK, BLK), BLK)
-    qs = pl.ds(pl.multiple_of(qi * BLK, BLK), BLK)
+def attn_bwd_tile(ki, size, qj, diag, ct, nat, nat_q, nat_do, dot_t, stat, dqt, dkv):
+    ks = pl.ds(pl.multiple_of(ki * size, size), size)
+    qs = pl.ds(pl.multiple_of(qj * HALF, HALF), HALF)
     for h in range(4):
         s = nn(nat[2 * h, ks, :], ct[3 * h * 64:3 * h * 64 + 64, qs])
         r = nn(nat[2 * h + 1, ks, :], dot_t[h * 64:(h + 1) * 64, qs])
         p = jnp.exp2((s - stat[h:h + 1, qs]) * LOG2E) * stat[4 + h:5 + h, qs]
         if diag:
-            key = lax.broadcasted_iota(jnp.int32, (BLK, BLK), 0)
-            query = lax.broadcasted_iota(jnp.int32, (BLK, BLK), 1)
+            key = lax.broadcasted_iota(jnp.int32, (size, HALF), 0)
+            query = lax.broadcasted_iota(jnp.int32, (size, HALF), 1)
             p = jnp.where(key <= query, p, 0.0)
         ds = (p * (r - stat[8 + h:9 + h, qs])).astype(BF16)
         dkv[h, ks, :] += nn(p.astype(BF16), nat_do[h, qs, :]) + nn(ds, nat_q[h, qs, :])
@@ -194,17 +194,20 @@
         ref = e_half(pair, part_no)
         return send(ref, ref, ssem.at[21 + part_no], rsem.at[21 + part_no], pair)
 
-    def e_peer(n):
-        ref = e_half(chip * 2 + 1 - n, core)
-        return send(ref, ref, ssem.at[23 + n], rsem.at[23 + n], peer)
-
-    def from_peer(n):
-        ref = e_half((1 - chip) * 2 + 1 - n, core)
-        return send(ref, ref, ssem.at[23 + n], rsem.at[23 + n], peer)
-
-    def relay(n, part_no):
-        ref = e_half((1 - chip) * 2 + 1 - n, part_no)
-        return send(ref, ref, ssem.at[25 + n], rsem.at[25 + n], pair)
+    def e_chunk(block, part_no, who):
+        return e.at[rows(block * BLK + part_no * HALF + who * 128, 128), :]
+
+    def e_peer(j):
+        ref = e_chunk(chip * 2 + 1 - j // 2, j % 2, core)
+        return send(ref, ref, ssem.at[23 + j], rsem.at[23 + j], peer)
+
+    def from_peer(j):
+        ref = e_chunk((1 - chip) * 2 + 1 - j // 2, j % 2, core)
+        return send(ref, ref, ssem.at[23 + j], rsem.at[23 + j], peer)
+
+    def relay(j, who):
+        ref = e_chunk((1 - chip) * 2 + 1 - j // 2, j % 2, who)
+        return send(ref, ref, ssem.at[33 + j], rsem.at[33 + j], pair)
 
     w_swap = send(wqkvt, w_pair, ssem.at[29], rsem.at[29], pair)
 
@@ -366,19 +369,24 @@
             e[rows_n, :] = grad.astype(BF16)
             e_pair(n).start()
 
-            @pl.when(core == n)
-            def _():
-                @pl.when(core == 1)
-                def _():
-                    e_peer(0).start()
-
-                from_pair(core).wait_recv()
-
-                @pl.when(core == 0)
-                def _():
-                    e_peer(0).start()
-
+            @pl.when(n * core == 1)
+            def _():
                 e_peer(1).start()
+
+            from_pair(n).wait_recv()
+
+            @pl.when(n == 0)
+            def _():
+                e_peer(0).start()
+
+            @pl.when(n * (1 - core) == 1)
+            def _():
+                e_peer(1).start()
+
+            @pl.when(n == 1)
+            def _():
+                e_peer(2).start()
+                e_peer(3).start()
 
     pl.run_scoped(
         phase_one,
@@ -400,14 +408,13 @@
         l_x.start()
         dkv[...] = jnp.zeros_like(dkv)
         dqt[...] = jnp.zeros_like(dqt)
-        from_pair(1 - core).wait_recv()
         for n in range(2):
             d2_far(n).wait_send()
         l_wo.wait()
 
-        @pl.loop(0, 2)
+        @pl.loop(0, 4)
         def _(n):
-            do_block(chip * 2 + n, e, wo, ot, dot_t, nat_do, stat)
+            do_block(chip * 4 + n, e, wo, ot, dot_t, nat_do, stat)
 
         w_swap.wait_recv()
 
@@ -418,31 +425,39 @@
         def d1_far(n):
             return send(d2_send.at[n], d1_recv.at[core], ssem.at[30 + n], rsem.at[30 + core], (1 - chip) * 2 + 1 - n)
 
-        @pl.loop(0, 6)
+        @pl.loop(0, 12)
         def _(i):
-            group = i // 2
+            group = i // 4
             far = group % 2
-            n = i - 2 * group
+            j = i - 4 * group
+            n = j // 2
+            odd = j - 2 * n
             qi = (1 - far) * (chip * 2 + n) + far * ((1 - chip) * 2 + 1 - n)
+            qj = qi * 2 + odd
             low = (group // 2) * chip * 2
             high = far * qi + (1 - far) * ((1 - group // 2) * ((1 - chip) * qi + chip * 2) + (group // 2) * chip * qi)
+            with_diag = far + (1 - far) * ((1 - group // 2) * (1 - chip) + (group // 2) * chip)
 
             @pl.when(far == 1)
             def _():
-                from_peer(n).wait_recv()
-                relay(n, core).start()
-                relay(n, 1 - core).wait_recv()
-                do_block(qi, e, wo, ot, dot_t, nat_do, stat)
+                from_peer(j).wait_recv()
+                relay(j, core).start()
+                relay(j, 1 - core).wait_recv()
+                do_block(qj, e, wo, ot, dot_t, nat_do, stat)
 
             @pl.loop(low, high)
             def _(ki):
-                attn_bwd_tile(ki, qi, False, ct, nat, nat_q, nat_do, dot_t, stat, dqt, dkv)
-
-            @pl.when(far + (1 - far) * ((1 - group // 2) * (1 - chip) + (group // 2) * chip) == 1)
-            def _():
-                attn_bwd_tile(qi, qi, True, ct, nat, nat_q, nat_do, dot_t, stat, dqt, dkv)
-
-            @pl.when(far == 1)
+                attn_bwd_tile(ki, BLK, qj, False, ct, nat, nat_q, nat_do, dot_t, stat, dqt, dkv)
+
+            @pl.when(with_diag * odd == 1)
+            def _():
+                attn_bwd_tile(qj - 1, HALF, qj, False, ct, nat, nat_q, nat_do, dot_t, stat, dqt, dkv)
+
+            @pl.when(with_diag == 1)
+            def _():
+                attn_bwd_tile(qj, HALF, qj, True, ct, nat, nat_q, nat_do, dot_t, stat, dqt, dkv)
+
+            @pl.when(far * odd == 1)
             def _():
                 pack_dc(qi, dqt, dkv, dct)
                 swap_far(n, 1 - core).start()
@@ -481,10 +496,11 @@
             dx[sl, :] = (dh1[sl, :] + ln_backward(hat, rstd, g1[...], grad)).astype(BF16)
 
         outs[2].start()
+        for j in range(4):
+            e_peer(j).wait_send()
+            relay(j, core).wait_send()
         for n in range(2):
             e_pair(n).wait_send()
-            e_peer(n).wait_send()
-            relay(n, core).wait_send()
             swap_far(n, 1 - core).wait_send()
             d1_far(n).wait_send()
         w_swap.wait_send()
@@ -540,8 +556,8 @@
             vmem((256, tokens), F32),
             vmem((16, tokens), F32),
             pltpu.SemaphoreType.DMA((13,)),
-            pltpu.SemaphoreType.DMA((33,)),
-            pltpu.SemaphoreType.DMA((33,)),
+            pltpu.SemaphoreType.DMA((37,)),
+            pltpu.SemaphoreType.DMA((37,)),
             pltpu.SemaphoreType.REGULAR,
         ],
         compiler_params=pltpu.CompilerParams(collective_id=0, has_side_effects=True, vmem_limit_bytes=67043328),

time: 162 us -> 167 us (1.031)
  Pallas kernels: 153 us -> 158 us
    pallas_call x1, Pallas kernels: 153 us -> 158 us  [layer_grads(): pl.pallas_call(layer_kernel, name='layer_grads', out_shape=(shape((BLK, 1...]
where the time goes in v2:
time: 167 us
  Pallas kernels  158 us (95%)
  local copies, waits for them, and re-layouts  8.38 us (5%)
    pallas_call x1, Pallas kernels, layer_grads(): pl.pallas_call(layer_kernel, name='layer_grads', out_shape=(shape((BLK, 1...  158 us
    unnamed x13, local copies, waits for them, and re-layouts  8.38 us

profile of v2, /device:TPU:2, one launch (start us, length us, event | category | flops | bytes accessed | tf_op | source)
XLA Modules:
  0.0 166.9 jit_solution(259633084195110602)
XLA Ops:
  0.6 157.8 %layer_grads.1 = (bf16[512,1024]{1,0:T(8,128)(2,1)}, bf16[1024,768]{1,0:T(8,128)(2,1)}, bf16[256,1024]{1,0:T(8,128)(2,1)}, bf16[1024,1024]{1,0:T(8,128)(2,1)}, bf16[1024,1024]{1,0:T(8,128)(2,1)}) custom-call(bf16[512,1024]{1,0:T(8,128)(2,1)} %h1_hbm.1, bf16[512,1024]{1,0:T(8,128)(2,1)} %dy_hbm.1, bf16[512,1024]{1,0:T(8,128)(2,1)} %x_hbm.1, ...), custom_call_target="tpu_custom_call" | custom-call | flops 80000000000 | bytes 40000000 | tf_op jit(solution)/shard_map/layer_grads/pallas_call | solution.py:533
  158.5 0.0 copy-start.2
  158.5 2.4 %copy.19 = bf16[512,1024]{1,0:T(8,128)(2,1)} copy(bf16[512,1024]{1,0:T(8,128)(2,1)} %get-tuple-element.20) | data formatting | bytes 2097152
  160.9 0.0 copy-done.2
  160.9 0.0 copy-start.3
  160.9 0.0 copy-start.1
  160.9 1.1 copy.20
  162.0 0.2 copy-done.3
  162.2 0.8 copy.21
  163.0 0.2 copy-done.1
  163.2 0.0 copy-start
  163.2 1.3 copy.22
  164.5 1.0 copy-done
  165.6 1.3 copy.23
Async XLA Ops:
  158.5 2.4 %copy-start.2 = (bf16[1024,768]{1,0:T(8,128)(2,1)S(1)}, bf16[1024,768]{1,0:T(8,128)(2,1)}, u32[]{:S(2)}) copy-start(bf16[1024,768]{1,0:T(8,128)(2,1)} %get-tuple-element.21) | copy-start | bytes 4718596
  160.9 1.4 copy-start.3
  160.9 2.3 %copy-start.1 = (bf16[1024,1024]{1,0:T(8,128)(2,1)S(1)}, bf16[1024,1024]{1,0:T(8,128)(2,1)}, u32[]{:S(2)}) copy-start(bf16[1024,1024]{1,0:T(8,128)(2,1)} %get-tuple-element.23) | copy-start | bytes 6291460
  163.2 2.3 %copy-start = (bf16[1024,1024]{1,0:T(8,128)(2,1)S(1)}, bf16[1024,1024]{1,0:T(8,128)(2,1)}, u32[]{:S(2)}) copy-start(bf16[1024,1024]{1,0:T(8,128)(2,1)} %get-tuple-element.24) | copy-start | bytes 6291460

commit v3 on v2

--- a/solution.py
+++ b/solution.py
@@ -99,16 +99,16 @@
         stat[8 + h:9 + h, sl] = jnp.sum(part.astype(F32) * ot[h * 64:(h + 1) * 64, sl], axis=0, keepdims=True)
 
 
-def attn_bwd_tile(ki, size, qj, diag, ct, nat, nat_q, nat_do, dot_t, stat, dqt, dkv):
-    ks = pl.ds(pl.multiple_of(ki * size, size), size)
-    qs = pl.ds(pl.multiple_of(qj * HALF, HALF), HALF)
+def attn_bwd_tile(k0, ksize, q0, qsize, diag, ct, nat, nat_q, nat_do, dot_t, stat, dqt, dkv):
+    ks = pl.ds(pl.multiple_of(k0, HALF), ksize)
+    qs = pl.ds(pl.multiple_of(q0, HALF), qsize)
     for h in range(4):
         s = nn(nat[2 * h, ks, :], ct[3 * h * 64:3 * h * 64 + 64, qs])
         r = nn(nat[2 * h + 1, ks, :], dot_t[h * 64:(h + 1) * 64, qs])
         p = jnp.exp2((s - stat[h:h + 1, qs]) * LOG2E) * stat[4 + h:5 + h, qs]
         if diag:
-            key = lax.broadcasted_iota(jnp.int32, (size, HALF), 0)
-            query = lax.broadcasted_iota(jnp.int32, (size, HALF), 1)
+            key = lax.broadcasted_iota(jnp.int32, (ksize, qsize), 0)
+            query = lax.broadcasted_iota(jnp.int32, (ksize, qsize), 1)
             p = jnp.where(key <= query, p, 0.0)
         ds = (p * (r - stat[8 + h:9 + h, qs])).astype(BF16)
         dkv[h, ks, :] += nn(p.astype(BF16), nat_do[h, qs, :]) + nn(ds, nat_q[h, qs, :])
@@ -425,39 +425,46 @@
         def d1_far(n):
             return send(d2_send.at[n], d1_recv.at[core], ssem.at[30 + n], rsem.at[30 + core], (1 - chip) * 2 + 1 - n)
 
-        @pl.loop(0, 12)
+        def take_far(n):
+            for half in range(2):
+                from_peer(2 * n + half).wait_recv()
+                relay(2 * n + half, core).start()
+
+        def far_do(n):
+            for half in range(2):
+                relay(2 * n + half, 1 - core).wait_recv()
+
+            @pl.loop(0, 2)
+            def _(half):
+                do_block(((1 - chip) * 2 + 1 - n) * 2 + half, e, wo, ot, dot_t, nat_do, stat)
+
+        @pl.loop(0, 6)
         def _(i):
-            group = i // 4
+            group = i // 2
             far = group % 2
-            j = i - 4 * group
-            n = j // 2
-            odd = j - 2 * n
+            n = i - 2 * group
             qi = (1 - far) * (chip * 2 + n) + far * ((1 - chip) * 2 + 1 - n)
-            qj = qi * 2 + odd
             low = (group // 2) * chip * 2
             high = far * qi + (1 - far) * ((1 - group // 2) * ((1 - chip) * qi + chip * 2) + (group // 2) * chip * qi)
-            with_diag = far + (1 - far) * ((1 - group // 2) * (1 - chip) + (group // 2) * chip)
+
+            @pl.when(i == 2)
+            def _():
+                take_far(0)
 
             @pl.when(far == 1)
             def _():
-                from_peer(j).wait_recv()
-                relay(j, core).start()
-                relay(j, 1 - core).wait_recv()
-                do_block(qj, e, wo, ot, dot_t, nat_do, stat)
+                far_do(n)
 
             @pl.loop(low, high)
             def _(ki):
-                attn_bwd_tile(ki, BLK, qj, False, ct, nat, nat_q, nat_do, dot_t, stat, dqt, dkv)
-
-            @pl.when(with_diag * odd == 1)
-            def _():
-                attn_bwd_tile(qj - 1, HALF, qj, False, ct, nat, nat_q, nat_do, dot_t, stat, dqt, dkv)
-
-            @pl.when(with_diag == 1)
-            def _():
-                attn_bwd_tile(qj, HALF, qj, True, ct, nat, nat_q, nat_do, dot_t, stat, dqt, dkv)
-
-            @pl.when(far * odd == 1)
+                attn_bwd_tile(ki * BLK, BLK, qi * BLK, BLK, False, ct, nat, nat_q, nat_do, dot_t, stat, dqt, dkv)
+
+            @pl.when(far + (1 - far) * ((1 - group // 2) * (1 - chip) + (group // 2) * chip) == 1)
+            def _():
+                attn_bwd_tile(qi * BLK, HALF, qi * BLK, BLK, True, ct, nat, nat_q, nat_do, dot_t, stat, dqt, dkv)
+                attn_bwd_tile(qi * BLK + HALF, HALF, qi * BLK + HALF, HALF, True, ct, nat, nat_q, nat_do, dot_t, stat, dqt, dkv)
+
+            @pl.when(far == 1)
             def _():
                 pack_dc(qi, dqt, dkv, dct)
                 swap_far(n, 1 - core).start()
@@ -465,6 +472,10 @@
                 swap_far(n, core).wait_recv()
                 d2_send[n] = (part[0:HALF, :] + nn(dct_far[n].T, w_pair[...])).astype(BF16)
                 d1_far(n).start()
+
+                @pl.when(n == 0)
+                def _():
+                    take_far(1)
 
         @pl.loop(0, 2)
         def _(n):
@@ -565,13 +576,40 @@
     )(h1, dy, x, g1, g2, wqkv, w1, w2, wo)
 
 
+def copy_kernel(*refs):
+    count = (len(refs) - 2) // 3
+    srcs, dsts, bufs, in_sem, out_sem = refs[:count], refs[count:2 * count], refs[2 * count:3 * count], refs[-2], refs[-1]
+    reads = [pltpu.make_async_copy(src, buf, in_sem.at[n]) for n, (src, buf) in enumerate(zip(srcs, bufs))]
+    writes = [pltpu.make_async_copy(buf, dst, out_sem.at[n]) for n, (dst, buf) in enumerate(zip(dsts, bufs))]
+    for copy in reads:
+        copy.start()
+    for read, write in zip(reads, writes):
+        read.wait()
+        write.start()
+    for copy in writes:
+        copy.wait()
+
+
+def copy_out(*arrays):
+    hbm = pl.BlockSpec(memory_space=pl.ANY)
+    return pl.pallas_call(
+        copy_kernel,
+        name="copy_out",
+        out_shape=[jax.ShapeDtypeStruct(a.shape, a.dtype) for a in arrays],
+        in_specs=[hbm] * len(arrays),
+        out_specs=[hbm] * len(arrays),
+        scratch_shapes=[pltpu.VMEM(a.shape, a.dtype) for a in arrays] + [pltpu.SemaphoreType.DMA((len(arrays),))] * 2,
+        compiler_params=pltpu.CompilerParams(vmem_limit_bytes=67043328),
+    )(*arrays)
+
+
 def solution(mesh):
     row_spec = P(('dp', 'tp'), None)
     in_specs = (row_spec, row_spec, row_spec, P(None), P(None), P(None, 'tp'), P('tp', None, None), P(None, 'tp'), P('tp', None))
     out_specs = (row_spec, P('dp', 'tp'), P(('dp', 'tp'), None, None), P('dp', 'tp'), P(('dp', 'tp'), None))
 
     def device_step(in_rows, mid_rows, gout_rows, ln1_gain, ln2_gain, wqkv_loc, wout_loc, wfc1_loc, wfc2_loc):
-        grad_in, grad_wqkv, grad_wout, grad_wfc1, grad_wfc2 = layer_grads(mid_rows, gout_rows, in_rows, ln1_gain.reshape(1, 1024), ln2_gain.reshape(1, 1024), wqkv_loc, wfc1_loc, wfc2_loc, wout_loc.reshape(256, 1024))
+        grad_in, grad_wqkv, grad_wout, grad_wfc1, grad_wfc2 = copy_out(*layer_grads(mid_rows, gout_rows, in_rows, ln1_gain.reshape(1, 1024), ln2_gain.reshape(1, 1024), wqkv_loc, wfc1_loc, wfc2_loc, wout_loc.reshape(256, 1024)))
         return grad_in, grad_wqkv, grad_wout.reshape(4, 64, 1024), grad_wfc1, grad_wfc2
 
     return jax.shard_map(device_step, mesh=mesh, in_specs=in_specs, out_specs=out_specs, check_vma=False)

time: 167 us -> 160 us (0.958)
  local copies, waits for them, and re-layouts: 8.38 us -> 0 us
    unnamed x13 -> x0, local copies, waits for them, and re-layouts: 8.38 us -> none
    pallas_call x0 -> x1, Pallas kernels: none -> 5.72 us  [copy_out(): pl.pallas_call(copy_kernel, name='copy_out', out_shape=[jax.ShapeDtypeStr...]
    pallas_call x1, Pallas kernels: 158 us -> 153 us  [layer_grads(): pl.pallas_call(layer_kernel, name='layer_grads', out_shape=(shape((BLK, 1...]
where the time goes in v3:
time: 160 us
  Pallas kernels  159 us (99%)
    pallas_call x1, Pallas kernels, layer_grads(): pl.pallas_call(layer_kernel, name='layer_grads', out_shape=(shape((BLK, 1...  153 us
    pallas_call x1, Pallas kernels, copy_out(): pl.pallas_call(copy_kernel, name='copy_out', out_shape=[jax.ShapeDtypeStr...  5.72 us

profile of v3, /device:TPU:2, one launch (start us, length us, event | category | flops | bytes accessed | tf_op | source)
XLA Modules:
  0.0 159.5 jit_solution(16721150471214387271)
XLA Ops:
  0.6 153.0 %layer_grads.1 = (bf16[512,1024]{1,0:T(8,128)(2,1)}, bf16[1024,768]{1,0:T(8,128)(2,1)}, bf16[256,1024]{1,0:T(8,128)(2,1)}, bf16[1024,1024]{1,0:T(8,128)(2,1)}, bf16[1024,1024]{1,0:T(8,128)(2,1)}) custom-call(bf16[512,1024]{1,0:T(8,128)(2,1)} %h1_hbm.1, bf16[512,1024]{1,0:T(8,128)(2,1)} %dy_hbm.1, bf16[512,1024]{1,0:T(8,128)(2,1)} %x_hbm.1, ...), custom_call_target="tpu_custom_call" | custom-call | flops 80000000000 | bytes 40000000 | tf_op jit(solution)/shard_map/layer_grads/pallas_call | solution.py:544
  153.6 5.7 %copy_out.1 = (bf16[512,1024]{1,0:T(8,128)(2,1)}, bf16[1024,768]{1,0:T(8,128)(2,1)}, bf16[256,1024]{1,0:T(8,128)(2,1)}, bf16[1024,1024]{1,0:T(8,128)(2,1)}, bf16[1024,1024]{1,0:T(8,128)(2,1)}) custom-call(bf16[512,1024]{1,0:T(8,128)(2,1)} %get-tuple-element.15.refs_0_, bf16[1024,768]{1,0:T(8,128)(2,1)} %get-tuple-element.16.refs_1_, ...), custom_call_target="tpu_custom_call" | custom-call | tf_op jit(solution)/shard_map/copy_out/pallas_call | solution.py:595

commit v4 on v3

--- a/solution.py
+++ b/solution.py
@@ -44,14 +44,13 @@
     return lax.dot_general(a, b, (((1,), (1,)), ((), ())), preferred_element_type=F32)
 
 
-def qkv_block(i, n1, wqkvt, ct, nat, nat_q):
+def qkv_block(i, n1, wqkvt, ct, nat):
     sl = pl.ds(pl.multiple_of(i * BLK, BLK), BLK)
     for n in range(4):
         c = nt(wqkvt[n * 192:(n + 1) * 192, :], n1[sl, :]).astype(BF16)
         q = c[0:64, :] * jnp.asarray(0.125, BF16)
         ct[n * 192:n * 192 + 64, sl] = q
         ct[n * 192 + 64:n * 192 + 192, sl] = c[64:192, :]
-        nat_q[n, sl, :] = jnp.concatenate([q, jnp.zeros_like(q)], axis=0).T
         nat[2 * n, sl, :] = c[64:128, :].T
         nat[2 * n + 1, sl, :] = c[128:192, :].T
 
@@ -89,17 +88,16 @@
         ot[h * 64:(h + 1) * 64, :] = ot[h * 64:(h + 1) * 64, :] * inv
 
 
-def do_block(i, e, wo, ot, dot_t, nat_do, stat):
+def do_block(i, e, wo, ot, dot_t, stat):
     sl = pl.ds(pl.multiple_of(i * HALF, HALF), HALF)
     d = nt(wo[...], e[sl, :]).astype(BF16)
     dot_t[:, sl] = d
     for h in range(4):
         part = d[h * 64:(h + 1) * 64, :]
-        nat_do[h, sl, :] = jnp.concatenate([jnp.zeros_like(part), part], axis=0).T
         stat[8 + h:9 + h, sl] = jnp.sum(part.astype(F32) * ot[h * 64:(h + 1) * 64, sl], axis=0, keepdims=True)
 
 
-def attn_bwd_tile(k0, ksize, q0, qsize, diag, ct, nat, nat_q, nat_do, dot_t, stat, dqt, dkv):
+def attn_bwd_tile(k0, ksize, q0, qsize, diag, ct, nat, dot_t, stat, dqt, dkt, dvt):
     ks = pl.ds(pl.multiple_of(k0, HALF), ksize)
     qs = pl.ds(pl.multiple_of(q0, HALF), qsize)
     for h in range(4):
@@ -111,16 +109,18 @@
             query = lax.broadcasted_iota(jnp.int32, (ksize, qsize), 1)
             p = jnp.where(key <= query, p, 0.0)
         ds = (p * (r - stat[8 + h:9 + h, qs])).astype(BF16)
-        dkv[h, ks, :] += nn(p.astype(BF16), nat_do[h, qs, :]) + nn(ds, nat_q[h, qs, :])
         hs = slice(h * 64, (h + 1) * 64)
+        dvt[hs, ks] += nt(dot_t[hs, qs], p.astype(BF16))
+        dkt[hs, ks] += nt(ct[3 * h * 64:3 * h * 64 + 64, qs], ds)
         dqt[hs, qs] += nn(ct[(3 * h + 1) * 64:(3 * h + 2) * 64, ks], ds)
 
 
-def pack_dc(i, dqt, dkv, dct):
+def pack_dc(i, dqt, dkt, dvt, dct):
     sl = pl.ds(pl.multiple_of(i * BLK, BLK), BLK)
     for h in range(4):
         dct[3 * h * 64:3 * h * 64 + 64, sl] = (dqt[h * 64:(h + 1) * 64, sl] * 0.125).astype(BF16)
-        dct[(3 * h + 1) * 64:(3 * h + 3) * 64, sl] = dkv[h, sl, :].astype(BF16).T
+        dct[(3 * h + 1) * 64:(3 * h + 2) * 64, sl] = dkt[h * 64:(h + 1) * 64, sl].astype(BF16)
+        dct[(3 * h + 2) * 64:(3 * h + 3) * 64, sl] = dvt[h * 64:(h + 1) * 64, sl].astype(BF16)
 
 
 MESH_ID = pl.DeviceIdType.MESH
@@ -170,7 +170,7 @@
 
 def layer_kernel(h1_hbm, dy_hbm, x_hbm, g1, g2, wqkv_hbm, w1_hbm, w2_hbm, wo_hbm,
                  dx_hbm, dwqkv_hbm, dwo_hbm, dw1_hbm, dw2_hbm,
-                 n2, dy, n1, w1_pair, da_pair, d2_send, d2_recv, d1_recv, w_pair, dct_far, dct_own, wqkvt, dh1, ct, nat, nat_q, ot, stat,
+                 n2, dy, n1, w1_pair, da_pair, d2_send, d2_recv, d1_recv, w_pair, dct_far, dct_own, wqkvt, dh1, ct, nat, ot, stat,
                  lsem, ssem, rsem, free_sem):
     me, chip, core, pair, peer, diag = place()
     own = rows(me * BLK, BLK)
@@ -262,7 +262,7 @@
 
         @pl.loop(0, 2)
         def _(n):
-            qkv_block(chip * 2 + n, n1, wqkvt, ct, nat, nat_q)
+            qkv_block(chip * 2 + n, n1, wqkvt, ct, nat)
 
         w_swap.start()
 
@@ -331,7 +331,7 @@
                         for n in range(2):
                             chunk_copy(n1, diag, n, 14, pair).wait_recv()
 
-                    qkv_block(peer + j * (diag - peer), n1, wqkvt, ct, nat, nat_q)
+                    qkv_block(peer + j * (diag - peer), n1, wqkvt, ct, nat)
 
             group = i // 2
             far = group % 2
@@ -401,12 +401,13 @@
         dw2=pltpu.VMEM((1024, 1024), BF16),
     )
 
-    def phase_two(nat_do, dot_t, dqt, dkv, wo, part, x, dx, dwqkv, dwo, dct):
+    def phase_two(dot_t, dqt, dkt, dvt, wo, part, x, dx, dwqkv, dwo, dct):
         l_wo = pltpu.make_async_copy(wo_hbm, wo, lsem.at[8])
         l_wo.start()
         l_x = pltpu.make_async_copy(x_hbm, x, lsem.at[9])
         l_x.start()
-        dkv[...] = jnp.zeros_like(dkv)
+        dkt[...] = jnp.zeros_like(dkt)
+        dvt[...] = jnp.zeros_like(dvt)
         dqt[...] = jnp.zeros_like(dqt)
         for n in range(2):
             d2_far(n).wait_send()
@@ -414,7 +415,7 @@
 
         @pl.loop(0, 4)
         def _(n):
-            do_block(chip * 4 + n, e, wo, ot, dot_t, nat_do, stat)
+            do_block(chip * 4 + n, e, wo, ot, dot_t, stat)
 
         w_swap.wait_recv()
 
@@ -422,8 +423,9 @@
             block = (1 - chip) * 2 + 1 - n
             return send(dct.at[:, rows(block * BLK + mine_or_theirs * HALF, HALF)], dct_far.at[n], ssem.at[27 + n], rsem.at[27 + n], pair)
 
-        def d1_far(n):
-            return send(d2_send.at[n], d1_recv.at[core], ssem.at[30 + n], rsem.at[30 + core], (1 - chip) * 2 + 1 - n)
+        def d1_far(n, piece):
+            sl = rows(piece * 128, 128)
+            return send(d2_send.at[n, sl, :], d1_recv.at[core, sl, :], ssem.at[30 + n + 7 * piece], rsem.at[30 + core + 7 * piece], (1 - chip) * 2 + 1 - n)
 
         def take_far(n):
             for half in range(2):
@@ -436,7 +438,7 @@
 
             @pl.loop(0, 2)
             def _(half):
-                do_block(((1 - chip) * 2 + 1 - n) * 2 + half, e, wo, ot, dot_t, nat_do, stat)
+                do_block(((1 - chip) * 2 + 1 - n) * 2 + half, e, wo, ot, dot_t, stat)
 
         @pl.loop(0, 6)
         def _(i):
@@ -450,36 +452,39 @@
             @pl.when(i == 2)
             def _():
                 take_far(0)
-
-            @pl.when(far == 1)
-            def _():
-                far_do(n)
+                far_do(0)
 
             @pl.loop(low, high)
             def _(ki):
-                attn_bwd_tile(ki * BLK, BLK, qi * BLK, BLK, False, ct, nat, nat_q, nat_do, dot_t, stat, dqt, dkv)
+                attn_bwd_tile(ki * BLK, BLK, qi * BLK, BLK, False, ct, nat, dot_t, stat, dqt, dkt, dvt)
 
             @pl.when(far + (1 - far) * ((1 - group // 2) * (1 - chip) + (group // 2) * chip) == 1)
             def _():
-                attn_bwd_tile(qi * BLK, HALF, qi * BLK, BLK, True, ct, nat, nat_q, nat_do, dot_t, stat, dqt, dkv)
-                attn_bwd_tile(qi * BLK + HALF, HALF, qi * BLK + HALF, HALF, True, ct, nat, nat_q, nat_do, dot_t, stat, dqt, dkv)
+                attn_bwd_tile(qi * BLK, HALF, qi * BLK, BLK, True, ct, nat, dot_t, stat, dqt, dkt, dvt)
+                attn_bwd_tile(qi * BLK + HALF, HALF, qi * BLK + HALF, HALF, True, ct, nat, dot_t, stat, dqt, dkt, dvt)
 
             @pl.when(far == 1)
             def _():
-                pack_dc(qi, dqt, dkv, dct)
+                pack_dc(qi, dqt, dkt, dvt, dct)
                 swap_far(n, 1 - core).start()
                 part[0:HALF, :] = nn(dct[:, rows(qi * BLK + core * HALF, HALF)].T, wqkvt[...])
-                swap_far(n, core).wait_recv()
-                d2_send[n] = (part[0:HALF, :] + nn(dct_far[n].T, w_pair[...])).astype(BF16)
-                d1_far(n).start()
 
                 @pl.when(n == 0)
                 def _():
                     take_far(1)
+                    far_do(1)
+
+                swap_far(n, core).wait_recv()
+
+                @pl.loop(0, 2)
+                def _(piece):
+                    sl = rows(piece * 128, 128)
+                    d2_send[n, sl, :] = (part[sl, :] + nn(dct_far[n, :, sl].T, w_pair[...])).astype(BF16)
+                    d1_far(n, piece).start()
 
         @pl.loop(0, 2)
         def _(n):
-            pack_dc(chip * 2 + n, dqt, dkv, dct)
+            pack_dc(chip * 2 + n, dqt, dkt, dvt, dct)
 
         swap = send(dct.at[:, rows(pair * BLK, BLK)], dct_own, ssem.at[32], rsem.at[32], pair)
         swap.start()
@@ -493,39 +498,47 @@
             dwo[:, sl] = nn(ot[...].astype(BF16), e[:, sl]).astype(BF16)
             dwqkv[sl, :] = nn(dct[...], n1[:, sl]).astype(BF16).T
 
-        outs = [pltpu.make_async_copy(src, dst, lsem.at[10 + n]) for n, (src, dst) in enumerate(((dwqkv, dwqkv_hbm), (dwo, dwo_hbm), (dx, dx_hbm)))]
+        outs = [pltpu.make_async_copy(src, dst, lsem.at[10 + n]) for n, (src, dst) in enumerate(((dwqkv, dwqkv_hbm), (dwo, dwo_hbm)))]
         outs[0].start()
         outs[1].start()
         l_x.wait()
 
-        @pl.loop(0, 2)
-        def _(n):
-            send(d2_send.at[n], d1_recv.at[n], ssem.at[30 + n], rsem.at[30 + n], peer).wait_recv()
-            sl = rows(n * HALF, HALF)
+        def dx_out(k):
+            sl = rows(k * 128, 128)
+            return pltpu.make_async_copy(dx.at[sl, :], dx_hbm.at[sl, :], lsem.at[12 + k])
+
+        @pl.loop(0, 4)
+        def _(i):
+            piece = i // 2
+            n = i - 2 * piece
+            arrived = rows(piece * 128, 128)
+            send(d2_send.at[n, arrived, :], d1_recv.at[n, arrived, :], ssem.at[30 + n + 7 * piece], rsem.at[30 + n + 7 * piece], peer).wait_recv()
+            sl = rows(n * HALF + piece * 128, 128)
             hat, rstd = ln_forward(x[sl, :].astype(F32))
-            grad = part[sl, :] + d1_recv[n].astype(F32)
+            grad = part[sl, :] + d1_recv[n, arrived, :].astype(F32)
             dx[sl, :] = (dh1[sl, :] + ln_backward(hat, rstd, g1[...], grad)).astype(BF16)
-
-        outs[2].start()
+            dx_out(n * 2 + piece).start()
+
         for j in range(4):
             e_peer(j).wait_send()
             relay(j, core).wait_send()
         for n in range(2):
             e_pair(n).wait_send()
             swap_far(n, 1 - core).wait_send()
-            d1_far(n).wait_send()
+            for piece in range(2):
+                d1_far(n, piece).wait_send()
         w_swap.wait_send()
         swap.wait_send()
-        for copy in outs:
+        for copy in outs + [dx_out(k) for k in range(4)]:
             copy.wait()
 
     tokens = 4 * BLK
     pl.run_scoped(
         phase_two,
-        nat_do=pltpu.VMEM((4, tokens, 128), BF16),
         dot_t=pltpu.VMEM((256, tokens), BF16),
         dqt=pltpu.VMEM((256, tokens), F32),
-        dkv=pltpu.VMEM((4, tokens, 128), F32),
+        dkt=pltpu.VMEM((256, tokens), F32),
+        dvt=pltpu.VMEM((256, tokens), F32),
         wo=pltpu.VMEM((256, 1024), BF16),
         part=pltpu.VMEM((BLK, 1024), F32),
         x=pltpu.VMEM((BLK, 1024), BF16),
@@ -563,12 +576,11 @@
             vmem((BLK, 1024), F32),
             vmem((768, tokens), BF16),
             vmem((8, tokens, 64), BF16),
-            vmem((4, tokens, 128), BF16),
             vmem((256, tokens), F32),
             vmem((16, tokens), F32),
-            pltpu.SemaphoreType.DMA((13,)),
-            pltpu.SemaphoreType.DMA((37,)),
-            pltpu.SemaphoreType.DMA((37,)),
+            pltpu.SemaphoreType.DMA((16,)),
+            pltpu.SemaphoreType.DMA((39,)),
+            pltpu.SemaphoreType.DMA((39,)),
             pltpu.SemaphoreType.REGULAR,
         ],
         compiler_params=pltpu.CompilerParams(collective_id=0, has_side_effects=True, vmem_limit_bytes=67043328),

time: 160 us -> 158 us (0.988)
  Pallas kernels: 159 us -> 157 us
    pallas_call x1, Pallas kernels: 153 us -> 151 us  [layer_grads(): pl.pallas_call(layer_kernel, name='layer_grads', out_shape=(shape((BLK, 1...]
where the time goes in v4:
time: 158 us
  Pallas kernels  157 us (99%)
    pallas_call x1, Pallas kernels, layer_grads(): pl.pallas_call(layer_kernel, name='layer_grads', out_shape=(shape((BLK, 1...  151 us
    pallas_call x1, Pallas kernels, copy_out(): pl.pallas_call(copy_kernel, name='copy_out', out_shape=[jax.ShapeDtypeStr...  5.72 us

profile of v4, /device:TPU:2, one launch (start us, length us, event | category | flops | bytes accessed | tf_op | source)
XLA Modules:
  0.0 157.9 jit_solution(3571223436238246381)
XLA Ops:
  0.6 151.4 %layer_grads.1 = (bf16[512,1024]{1,0:T(8,128)(2,1)}, bf16[1024,768]{1,0:T(8,128)(2,1)}, bf16[256,1024]{1,0:T(8,128)(2,1)}, bf16[1024,1024]{1,0:T(8,128)(2,1)}, bf16[1024,1024]{1,0:T(8,128)(2,1)}) custom-call(bf16[512,1024]{1,0:T(8,128)(2,1)} %h1_hbm.1, bf16[512,1024]{1,0:T(8,128)(2,1)} %dy_hbm.1, bf16[512,1024]{1,0:T(8,128)(2,1)} %x_hbm.1, ...), custom_call_target="tpu_custom_call" | custom-call | flops 80000000000 | bytes 40000000 | tf_op jit(solution)/shard_map/layer_grads/pallas_call | solution.py:557
  152.0 5.7 %copy_out.1 = (bf16[512,1024]{1,0:T(8,128)(2,1)}, bf16[1024,768]{1,0:T(8,128)(2,1)}, bf16[256,1024]{1,0:T(8,128)(2,1)}, bf16[1024,1024]{1,0:T(8,128)(2,1)}, bf16[1024,1024]{1,0:T(8,128)(2,1)}) custom-call(bf16[512,1024]{1,0:T(8,128)(2,1)} %get-tuple-element.15.refs_0_, bf16[1024,768]{1,0:T(8,128)(2,1)} %get-tuple-element.16.refs_1_, ...), custom_call_target="tpu_custom_call" | custom-call | tf_op jit(solution)/shard_map/copy_out/pallas_call | solution.py:607

commit v5 on v4

--- a/solution.py
+++ b/solution.py
@@ -215,16 +215,20 @@
         local = []
         for n, (src, dst) in enumerate(((dy_hbm, dy.at[own, :]), (h1_hbm, h1), (x_hbm, x), (w1_hbm, w1), (w2_hbm, dw2), (wqkv_hbm, wqkv))):
             copy = pltpu.make_async_copy(src, dst, lsem.at[n])
-            copy.start()
             local.append(copy)
         l_dy, l_h1, l_x, l_w1, l_w2, l_wqkv = local
+        for copy in (l_dy, l_h1, l_x):
+            copy.start()
 
         entry_barrier((pair, peer, diag))
 
+        first_rows = rows(me * BLK, HALF)
+        send(dy_hbm.at[0:HALF, :], dy.at[first_rows, :], ssem.at[6], rsem.at[6], peer).start()
+        for copy in (l_w1, l_w2, l_wqkv):
+            copy.start()
         to_pair = [send(ref.at[own, :], ref.at[own, :], ssem.at[n], rsem.at[n], pair) for n, ref in enumerate((n2, dy, n1))]
         to_pair.append(send(w1, w1_pair, ssem.at[3], rsem.at[3], pair))
         l_dy.wait()
-        chunk_copy(dy, me, 0, 6, peer).start()
         to_pair[1].start()
         l_h1.wait()
         ln_rows(h1, g2, n2, me * BLK)
@@ -469,11 +473,6 @@
                 swap_far(n, 1 - core).start()
                 part[0:HALF, :] = nn(dct[:, rows(qi * BLK + core * HALF, HALF)].T, wqkvt[...])
 
-                @pl.when(n == 0)
-                def _():
-                    take_far(1)
-                    far_do(1)
-
                 swap_far(n, core).wait_recv()
 
                 @pl.loop(0, 2)
@@ -481,6 +480,11 @@
                     sl = rows(piece * 128, 128)
                     d2_send[n, sl, :] = (part[sl, :] + nn(dct_far[n, :, sl].T, w_pair[...])).astype(BF16)
                     d1_far(n, piece).start()
+
+                @pl.when(n == 0)
+                def _():
+                    take_far(1)
+                    far_do(1)
 
         @pl.loop(0, 2)
         def _(n):

time: 158 us -> 158 us (level)
  no operation moved by 1% of the time
where the time goes in v5:
time: 158 us; the launch traced here: 157 us
  Pallas kernels  157 us (99%)
    pallas_call x1, Pallas kernels, layer_grads(): pl.pallas_call(layer_kernel, name='layer_grads', out_shape=(shape((BLK, 1...  151 us
    pallas_call x1, Pallas kernels, copy_out(): pl.pallas_call(copy_kernel, name='copy_out', out_shape=[jax.ShapeDtypeStr...  5.72 us

profile of v5, /device:TPU:2, one launch (start us, length us, event | category | flops | bytes accessed | tf_op | source)
XLA Modules:
  0.0 157.4 jit_solution(8401008870975335207)
XLA Ops:
  0.6 150.9 %layer_grads.1 = (bf16[512,1024]{1,0:T(8,128)(2,1)}, bf16[1024,768]{1,0:T(8,128)(2,1)}, bf16[256,1024]{1,0:T(8,128)(2,1)}, bf16[1024,1024]{1,0:T(8,128)(2,1)}, bf16[1024,1024]{1,0:T(8,128)(2,1)}) custom-call(bf16[512,1024]{1,0:T(8,128)(2,1)} %h1_hbm.1, bf16[512,1024]{1,0:T(8,128)(2,1)} %dy_hbm.1, bf16[512,1024]{1,0:T(8,128)(2,1)} %x_hbm.1, ...), custom_call_target="tpu_custom_call" | custom-call | flops 80000000000 | bytes 40000000 | tf_op jit(solution)/shard_map/layer_grads/pallas_call | solution.py:561
  151.5 5.7 %copy_out.1 = (bf16[512,1024]{1,0:T(8,128)(2,1)}, bf16[1024,768]{1,0:T(8,128)(2,1)}, bf16[256,1024]{1,0:T(8,128)(2,1)}, bf16[1024,1024]{1,0:T(8,128)(2,1)}, bf16[1024,1024]{1,0:T(8,128)(2,1)}) custom-call(bf16[512,1024]{1,0:T(8,128)(2,1)} %get-tuple-element.15.refs_0_, bf16[1024,768]{1,0:T(8,128)(2,1)} %get-tuple-element.16.refs_1_, ...), custom_call_target="tpu_custom_call" | custom-call | tf_op jit(solution)/shard_map/copy_out/pallas_call | solution.py:611

commit v6 on v5

--- a/solution.py
+++ b/solution.py
@@ -306,8 +306,39 @@
 
         outs = [pltpu.make_async_copy(src, dst, lsem.at[6 + n]) for n, (src, dst) in enumerate(((dw1, dw1_hbm), (dw2, dw2_hbm)))]
 
+        def mid_grad(n):
+            d2_far(n).wait_recv()
+            sl = rows(n * HALF, HALF)
+            hat, rstd = ln_forward(h1[sl, :].astype(F32))
+            rows_n = rows(me * BLK + n * HALF, HALF)
+            grad = dy[rows_n, :].astype(F32) + ln_backward(hat, rstd, g2[...], dh1[sl, :] + d2_recv[n].astype(F32))
+            dh1[sl, :] = grad
+            e[rows_n, :] = grad.astype(BF16)
+            e_pair(n).start()
+            if n == 0:
+                from_pair(0).wait_recv()
+                e_peer(0).start()
+            else:
+                @pl.when(core == 1)
+                def _():
+                    e_peer(1).start()
+
+                from_pair(1).wait_recv()
+
+                @pl.when(core == 0)
+                def _():
+                    e_peer(1).start()
+
+                e_peer(2).start()
+                e_peer(3).start()
+
         @pl.loop(0, 6)
         def _(i):
+            @pl.when(i == 4)
+            def _():
+                pl.semaphore_wait(free_sem, 2)
+                mid_grad(0)
+
             @pl.when(i == 2)
             def _():
                 @pl.loop(0, 4)
@@ -360,37 +391,7 @@
             for ref, block, first, to in ((dy, me, 6, peer), (n1, me, 8, peer), (dy, peer, 12, pair), (n1, peer, 14, pair)):
                 chunk_copy(ref, block, n, first, to).wait_send()
             da_far(n).wait_send()
-        pl.semaphore_wait(free_sem, 2)
-
-        @pl.loop(0, 2)
-        def _(n):
-            d2_far(n).wait_recv()
-            sl = rows(n * HALF, HALF)
-            hat, rstd = ln_forward(h1[sl, :].astype(F32))
-            rows_n = rows(me * BLK + n * HALF, HALF)
-            grad = dy[rows_n, :].astype(F32) + ln_backward(hat, rstd, g2[...], dh1[sl, :] + d2_recv[n].astype(F32))
-            dh1[sl, :] = grad
-            e[rows_n, :] = grad.astype(BF16)
-            e_pair(n).start()
-
-            @pl.when(n * core == 1)
-            def _():
-                e_peer(1).start()
-
-            from_pair(n).wait_recv()
-
-            @pl.when(n == 0)
-            def _():
-                e_peer(0).start()
-
-            @pl.when(n * (1 - core) == 1)
-            def _():
-                e_peer(1).start()
-
-            @pl.when(n == 1)
-            def _():
-                e_peer(2).start()
-                e_peer(3).start()
+        mid_grad(1)
 
     pl.run_scoped(
         phase_one,
@@ -467,6 +468,10 @@
                 attn_bwd_tile(qi * BLK, HALF, qi * BLK, BLK, True, ct, nat, dot_t, stat, dqt, dkt, dvt)
                 attn_bwd_tile(qi * BLK + HALF, HALF, qi * BLK + HALF, HALF, True, ct, nat, dot_t, stat, dqt, dkt, dvt)
 
+            @pl.when(i == 2)
+            def _():
+                take_far(1)
+
             @pl.when(far == 1)
             def _():
                 pack_dc(qi, dqt, dkt, dvt, dct)
@@ -483,7 +488,6 @@
 
                 @pl.when(n == 0)
                 def _():
-                    take_far(1)
                     far_do(1)
 
         @pl.loop(0, 2)

time: 158 us -> 157 us (level)
  Pallas kernels: 157 us -> 155 us
where the time goes in v6:
time: 157 us; the launch traced here: 156 us
  Pallas kernels  155 us (99%)
    pallas_call x1, Pallas kernels, layer_grads(): pl.pallas_call(layer_kernel, name='layer_grads', out_shape=(shape((BLK, 1...  149 us
    pallas_call x1, Pallas kernels, copy_out(): pl.pallas_call(copy_kernel, name='copy_out', out_shape=[jax.ShapeDtypeStr...  5.72 us

profile of v6, /device:TPU:2, one launch (start us, length us, event | category | flops | bytes accessed | tf_op | source)
XLA Modules:
  0.0 155.9 jit_solution(12958909232016229605)
XLA Ops:
  0.6 149.3 %layer_grads.1 = (bf16[512,1024]{1,0:T(8,128)(2,1)}, bf16[1024,768]{1,0:T(8,128)(2,1)}, bf16[256,1024]{1,0:T(8,128)(2,1)}, bf16[1024,1024]{1,0:T(8,128)(2,1)}, bf16[1024,1024]{1,0:T(8,128)(2,1)}) custom-call(bf16[512,1024]{1,0:T(8,128)(2,1)} %h1_hbm.1, bf16[512,1024]{1,0:T(8,128)(2,1)} %dy_hbm.1, bf16[512,1024]{1,0:T(8,128)(2,1)} %x_hbm.1, ...), custom_call_target="tpu_custom_call" | custom-call | flops 80000000000 | bytes 40000000 | tf_op jit(solution)/shard_map/layer_grads/pallas_call | solution.py:565
  150.0 5.7 %copy_out.1 = (bf16[512,1024]{1,0:T(8,128)(2,1)}, bf16[1024,768]{1,0:T(8,128)(2,1)}, bf16[256,1024]{1,0:T(8,128)(2,1)}, bf16[1024,1024]{1,0:T(8,128)(2,1)}, bf16[1024,1024]{1,0:T(8,128)(2,1)}) custom-call(bf16[512,1024]{1,0:T(8,128)(2,1)} %get-tuple-element.15.refs_0_, bf16[1024,768]{1,0:T(8,128)(2,1)} %get-tuple-element.16.refs_1_, ...), custom_call_target="tpu_custom_call" | custom-call | tf_op jit(solution)/shard_map/copy_out/pallas_call | solution.py:615
